TPU v7x, 8 devices: a whole 2x2x1 slice. The times are simulated.
8 devices in a mesh: dp: 1 (over z), tp: 8 (over y, x, core).
Axes of the slice: x: 2, y: 2, z: 1, core: 2. Of those that a mesh axis runs over, the one named last changes fastest.
Arguments:
- hidden: bfloat16 [2, 4096, 4096], P('dp', 'tp')
- lengths: int32 [2], P('dp')
- ln_gain: float32 [2, 4096], replicated
- ln_bias: float32 [2, 4096], replicated
- w_query: bfloat16 [2, 4096, 16, 256], P(None, None, 'tp')
- w_key: bfloat16 [2, 4096, 16, 256], P(None, None, 'tp')
- w_value: bfloat16 [2, 4096, 16, 256], P(None, None, 'tp')
- w_attn_out: bfloat16 [2, 16, 256, 4096], P(None, 'tp')
- w_fc_in: bfloat16 [2, 4096, 16384], P(None, None, 'tp')
- b_fc_in: float32 [2, 16384], P(None, 'tp')
- w_fc_out: bfloat16 [2, 16384, 4096], P(None, 'tp')
- b_fc_out: float32 [2, 4096], replicated
Outputs:
- output 1: bfloat16 [2, 4096, 4096], P('dp', 'tp')
- output 2: bfloat16 [2, 2, 16, 4096, 256], P(None, 'dp', 'tp')
- output 3: bfloat16 [2, 2, 16, 4096, 256], P(None, 'dp', 'tp')
All inputs are finite; a program needn't handle non-finite values.
Results may differ from a plain program's by a relative error of at most 0.0136841.
Values are sent between devices in bfloat16 or wider.
A program may use at most 1 GiB of HBM per device.

v0:
```python
import jax
import jax.numpy as jnp
from jax import lax
from jax.sharding import PartitionSpec as P, NamedSharding

ROTARY_DIM = 64
LN_EPS = 1e-5


def layer_norm(hidden_rows, gain_vec, bias_vec):
    rows_f32 = hidden_rows.astype(jnp.float32)
    row_mean = jnp.mean(rows_f32, axis=-1, keepdims=True)
    centered = rows_f32 - row_mean
    row_var = jnp.mean(centered * centered, axis=-1, keepdims=True)
    return (centered * lax.rsqrt(row_var + LN_EPS) * gain_vec + bias_vec).astype(jnp.bfloat16)


def rotary_tables(seq_full):
    positions = jnp.arange(seq_full).astype(jnp.float32)
    inv_freq = 10000.0 ** (-jnp.arange(0, ROTARY_DIM, 2).astype(jnp.float32) / ROTARY_DIM)
    angles = positions[:, None] * inv_freq[None, :]
    return jnp.cos(angles), jnp.sin(angles)


def apply_rotary(projected, cos_tab, sin_tab):
    lead_shape = projected.shape[:-1]
    pair_view = projected[..., :ROTARY_DIM].reshape(lead_shape + (ROTARY_DIM // 2, 2))
    even_part = pair_view[..., 0]
    odd_part = pair_view[..., 1]
    new_even = even_part * cos_tab - odd_part * sin_tab
    new_odd = odd_part * cos_tab + even_part * sin_tab
    rotated = jnp.stack([new_even, new_odd], axis=-1).reshape(lead_shape + (ROTARY_DIM,))
    return jnp.concatenate([rotated, projected[..., ROTARY_DIM:]], axis=-1)


def causal_attention(query_all, keys_all, values_all, lengths, block_count):
    seq_full = query_all.shape[2]
    block_len = seq_full // block_count
    score_scale = query_all.shape[3] ** -0.5
    key_pos = jnp.arange(seq_full)
    ctx_blocks = []
    for block_idx in range(block_count):
        start_at = block_idx * block_len
        stop_at = start_at + block_len
        q_pos = key_pos[start_at:stop_at]
        causal = key_pos[None, :stop_at] <= q_pos[:, None]
        in_len = key_pos[None, :stop_at] < lengths[:, None]
        allowed = causal[None, None, :, :] & in_len[:, None, None, :]
        scores = jnp.einsum("bhqe,bhke->bhqk", query_all[:, :, start_at:stop_at], keys_all[:, :, :stop_at], preferred_element_type=jnp.float32) * score_scale
        scores = jnp.where(allowed, scores, -1e30)
        attn_probs = jax.nn.softmax(scores, axis=-1).astype(jnp.bfloat16)
        ctx_blocks.append(jnp.einsum("bhqk,bhke->bhqe", attn_probs, values_all[:, :, :stop_at], preferred_element_type=jnp.float32).astype(jnp.bfloat16))
    return jnp.concatenate(ctx_blocks, axis=2)


def solution(mesh):
    tp_size = mesh.shape["tp"]

    def device_step(hidden, lengths, ln_gain, ln_bias, w_query, w_key, w_value, w_attn_out, w_fc_in, b_fc_in, w_fc_out, b_fc_out):
        seq_full = hidden.shape[1] * tp_size
        cos_tab, sin_tab = rotary_tables(seq_full)
        key_layers = []
        value_layers = []
        for layer_idx in range(w_query.shape[0]):
            normed = layer_norm(hidden, ln_gain[layer_idx], ln_bias[layer_idx])
            gathered = lax.all_gather(normed, "tp", axis=1, tiled=True)
            query_all = apply_rotary(jnp.einsum("btd,dhe->bhte", gathered, w_query[layer_idx], preferred_element_type=jnp.float32), cos_tab, sin_tab).astype(jnp.bfloat16)
            keys_all = apply_rotary(jnp.einsum("btd,dhe->bhte", gathered, w_key[layer_idx], preferred_element_type=jnp.float32), cos_tab, sin_tab).astype(jnp.bfloat16)
            values_all = jnp.einsum("btd,dhe->bhte", gathered, w_value[layer_idx], preferred_element_type=jnp.float32).astype(jnp.bfloat16)
            context = causal_attention(query_all, keys_all, values_all, lengths, tp_size)
            attn_part = jnp.einsum("bhte,hed->btd", context, w_attn_out[layer_idx], preferred_element_type=jnp.float32)
            fc_hidden = jax.nn.gelu(jnp.einsum("btd,df->btf", gathered, w_fc_in[layer_idx], preferred_element_type=jnp.float32) + b_fc_in[layer_idx], approximate=True).astype(jnp.bfloat16)
            mlp_part = jnp.einsum("btf,fd->btd", fc_hidden, w_fc_out[layer_idx], preferred_element_type=jnp.float32)
            branch_sum = (attn_part + mlp_part).astype(jnp.bfloat16)
            reduced = lax.psum_scatter(branch_sum, "tp", scatter_dimension=1, tiled=True)
            hidden = (hidden.astype(jnp.float32) + reduced.astype(jnp.float32) + b_fc_out[layer_idx]).astype(jnp.bfloat16)
            key_layers.append(keys_all)
            value_layers.append(values_all)
        return hidden, jnp.stack(key_layers), jnp.stack(value_layers)

    head_cols = P(None, None, "tp", None)
    cache_spec = P(None, "dp", "tp", None, None)
    return jax.shard_map(device_step, mesh=mesh, in_specs=(P("dp", "tp", None), P("dp"), P(), P(), head_cols, head_cols, head_cols, P(None, "tp", None, None), P(None, None, "tp"), P(None, "tp"), P(None, "tp", None), P()), out_specs=(P("dp", "tp", None), cache_spec, cache_spec), check_vma=False)
```

profile of v0, /device:TPU:0, one launch (start us, length us, event | category | flops | bytes accessed | tf_op | source)
XLA Modules:
  0.0 3250.5 jit_solution(3676620571337240765)
XLA Ops:
  22.6 8.4 fusion.423
  31.0 11.2 copy.90
  42.2 8.4 fusion.422
  50.6 11.2 copy.91
  100.6 221.9 %all-gather.3.cloned.1.call-done = bf16[2,4096,4096]{2,1,0:T(8,128)(2,1)} async-done(((bf16[2,512,4096]{2,1,0:T(8,128)(2,1)}), bf16[2,4096,4096]{2,1,0:T(8,128)(2,1)}) %all-gather.3.cloned.1.call-update) | async-done | bytes 67108880 | tf_op jit(solution)/shard_map/all_gather | solution.py:66
  322.6 44.4 %fusion.131 = f32[2,2,4096,256]{2,3,1,0:T(8,128)} fusion(bf16[2,4096,4096]{2,1,0:T(8,128)(2,1)} %all-gather.3.cloned.1.call-done, bf16[1,4096,2,256]{1,3,2,0:T(8,128)(2,1)} %copy.91), kind=kOutput, calls=%fused_computation.233 | convolution fusion | flops 34359738368 | bytes 88080384 | tf_op jit(solution)/shard_map/btd,dhe->bhte/dot_general | solution.py:68
  371.5 8.2 slice.834
  379.7 44.6 %fusion.128 = f32[2,2,4096,256]{2,3,1,0:T(8,128)} fusion(bf16[2,4096,4096]{2,1,0:T(8,128)(2,1)} %all-gather.3.cloned.1.call-done, bf16[1,4096,2,256]{1,3,2,0:T(8,128)(2,1)} %copy.90), kind=kOutput, calls=%fused_computation.232 | convolution fusion | flops 34359738368 | bytes 88080384 | tf_op jit(solution)/shard_map/btd,dhe->bhte/dot_general | solution.py:67
  429.0 8.2 slice.835
  505.6 8.7 fusion.186
  514.3 11.1 fusion.170
  525.4 13.4 fusion.160
  538.8 19.4 fusion.141
  566.3 13.6 fusion.429
  579.9 16.7 fusion.430
  596.6 21.0 fusion.431
  617.7 25.5 fusion.432
  643.2 29.8 fusion.433
  673.1 37.6 %fusion.434 = (f32[2,2,512]{2,1,0:T(2,128)}, f32[2,2,512,3584]{3,2,1,0:T(8,128)}) fusion(f32[2,2,512,3584]{3,2,1,0:T(8,128)} %fusion.160, pred[2,512,3584]{2,1,0:T(8,128)(4,1)} %broadcast_and_fusion.1), kind=kOutput, calls=%fused_computation.525 | output fusion | flops 44043776 | bytes 62398464 | tf_op jit(solution)/shard_map/sub | solution.py:51
  710.6 39.6 %fusion.435 = (f32[2,2,512]{2,1,0:T(2,128)}, f32[2,2,512,4096]{3,2,1,0:T(8,128)}) fusion(f32[2,2,512,4096]{3,2,1,0:T(8,128)} %fusion.141, pred[2,512,4096]{2,1,0:T(8,128)(4,1)} %broadcast_and_fusion), kind=kOutput, calls=%fused_computation.526 | output fusion | flops 50335744 | bytes 71311360 | tf_op jit(solution)/shard_map/sub | solution.py:51
  750.3 41.8 %fusion.150 = bf16[2,4096,2,256]{3,1,2,0:T(8,128)(2,1)S(1)} fusion(bf16[2,4096,4096]{2,1,0:T(8,128)(2,1)} %all-gather.3.cloned.1.call-done, bf16[1,4096,2,256]{3,2,1,0:T(2,128)(2,1)} %get-tuple-element.9), kind=kOutput, calls=%fused_computation.254 | convolution fusion | flops 34363932672 | bytes 79691776 | tf_op jit(solution)/shard_map/btd,dhe->bhte/dot_general | solution.py:69
  812.5 10.3 fusion.288
  822.9 11.2 fusion.282
  834.1 11.1 fusion.316
  845.1 14.6 fusion.310
  859.7 16.5 fusion.308
  876.2 51.7 %fusion.202 = f32[2,4096,4096,1]{2,1,3,0:T(8,128)} fusion(bf16[2,2,4096,256]{3,2,1,0:T(8,128)(2,1)} %fusion.308, bf16[2,2,256,4096]{3,2,1,0:T(8,128)(2,1)} %param.19), kind=kOutput, calls=%fused_computation.301 | convolution fusion | flops 34359738368 | bytes 146800640 | tf_op jit(solution)/shard_map/bhte,hed->btd/dot_general | solution.py:71
  927.9 151.4 %fusion.84 = f32[2,4096,2048]{2,1,0:T(8,128)} fusion(bf16[2,4096,4096]{2,1,0:T(8,128)(2,1)} %all-gather.3.cloned.1.call-done, bf16[2,4096,2048]{2,1,0:T(8,128)(2,1)} %param.20), kind=kOutput, calls=%fused_computation.146 | convolution fusion | flops 137438953472 | bytes 150994944 | tf_op jit(solution)/shard_map/btd,df->btf/dot_general | solution.py:72
  1079.2 166.6 %fusion.17 = bf16[2,4096,4096]{2,1,0:T(8,128)(2,1)} fusion(f32[2,4096,4096,1]{2,1,3,0:T(8,128)} %fusion.202, f32[2,4096,2048]{2,1,0:T(8,128)} %fusion.84, f32[2048]{0:T(1024)S(1)} %bitcast.207, bf16[2,2048,4096]{2,1,0:T(8,128)(2,1)} %param.22), kind=kOutput, calls=%fused_computation.19 | convolution fusion | flops 137673834496 | bytes 285220864 | tf_op jit(solution)/shard_map/btf,fd->btd/dot_general | solution.py:73
  1247.2 373.5 %reduce-scatter.3.cloned.1.call-done = bf16[2,512,4096]{2,1,0:T(8,128)(2,1)} async-done(((bf16[2,4096,4096]{2,1,0:T(8,128)(2,1)}), bf16[2,512,4096]{2,1,0:T(8,128)(2,1)}) %reduce-scatter.3.cloned.1.call-update) | async-done | bytes 8388624 | tf_op jit(solution)/shard_map/reduce_scatter | solution.py:75
  1637.6 11.7 copy.93
  1649.3 11.2 copy.94
  1660.5 274.4 %all-gather.5.cloned.1.call-done = bf16[2,4096,4096]{2,1,0:T(8,128)(2,1)} async-done(((bf16[2,512,4096]{2,1,0:T(8,128)(2,1)}), bf16[2,4096,4096]{2,1,0:T(8,128)(2,1)}) %all-gather.5.cloned.1.call-update) | async-done | bytes 67108880 | tf_op jit(solution)/shard_map/all_gather | solution.py:66
  1934.9 44.4 %fusion.137 = f32[2,2,4096,256]{2,3,1,0:T(8,128)} fusion(bf16[2,4096,4096]{2,1,0:T(8,128)(2,1)} %all-gather.5.cloned.1.call-done, bf16[1,4096,2,256]{1,3,2,0:T(8,128)(2,1)} %copy.94), kind=kOutput, calls=%fused_computation.235 | convolution fusion | flops 34359738368 | bytes 88080384 | tf_op jit(solution)/shard_map/btd,dhe->bhte/dot_general | solution.py:68
  1983.9 8.2 slice.832
  1992.1 44.6 %fusion.134 = f32[2,2,4096,256]{2,3,1,0:T(8,128)} fusion(bf16[2,4096,4096]{2,1,0:T(8,128)(2,1)} %all-gather.5.cloned.1.call-done, bf16[1,4096,2,256]{1,3,2,0:T(8,128)(2,1)} %copy.93), kind=kOutput, calls=%fused_computation.234 | convolution fusion | flops 34359738368 | bytes 88080384 | tf_op jit(solution)/shard_map/btd,dhe->bhte/dot_general | solution.py:67
  2041.3 8.2 slice.833
  2117.8 8.7 fusion.183
  2126.5 11.1 fusion.167
  2137.5 13.5 fusion.157
  2151.0 19.4 fusion.140
  2178.4 13.6 fusion.437
  2192.1 16.7 fusion.438
  2208.8 21.0 fusion.439
  2229.8 25.5 fusion.440
  2255.3 29.8 fusion.441
  2285.2 37.6 %fusion.442 = (f32[2,2,512]{2,1,0:T(2,128)}, f32[2,2,512,3584]{3,2,1,0:T(8,128)}) fusion(f32[2,2,512,3584]{3,2,1,0:T(8,128)} %fusion.157, pred[2,512,3584]{2,1,0:T(8,128)(4,1)} %broadcast_and_fusion.1), kind=kOutput, calls=%fused_computation.533 | output fusion | flops 44043776 | bytes 62398464 | tf_op jit(solution)/shard_map/sub | solution.py:51
  2322.8 39.6 %fusion.443 = (f32[2,2,512]{2,1,0:T(2,128)}, f32[2,2,512,4096]{3,2,1,0:T(8,128)}) fusion(f32[2,2,512,4096]{3,2,1,0:T(8,128)} %fusion.140, pred[2,512,4096]{2,1,0:T(8,128)(4,1)} %broadcast_and_fusion), kind=kOutput, calls=%fused_computation.534 | output fusion | flops 50335744 | bytes 71311360 | tf_op jit(solution)/shard_map/sub | solution.py:51
  2362.4 41.8 %fusion.153 = bf16[2,4096,2,256]{3,1,2,0:T(8,128)(2,1)S(1)} fusion(bf16[2,4096,4096]{2,1,0:T(8,128)(2,1)} %all-gather.5.cloned.1.call-done, bf16[1,4096,2,256]{3,2,1,0:T(2,128)(2,1)} %get-tuple-element.8), kind=kOutput, calls=%fused_computation.255 | convolution fusion | flops 34363932672 | bytes 79691776 | tf_op jit(solution)/shard_map/btd,dhe->bhte/dot_general | solution.py:69
  2424.7 10.3 fusion.291
  2435.0 11.2 fusion.285
  2446.2 11.1 fusion.319
  2457.3 14.6 fusion.313
  2471.8 16.5 fusion.309
  2488.3 51.7 %fusion.198 = f32[2,4096,4096,1]{2,1,3,0:T(8,128)} fusion(bf16[2,2,4096,256]{3,2,1,0:T(8,128)(2,1)} %fusion.309, bf16[2,2,256,4096]{3,2,1,0:T(8,128)(2,1)} %param.19), kind=kOutput, calls=%fused_computation.297 | convolution fusion | flops 34359738368 | bytes 146800640 | tf_op jit(solution)/shard_map/bhte,hed->btd/dot_general | solution.py:71
  2540.0 151.4 %fusion.81 = f32[2,4096,2048]{2,1,0:T(8,128)} fusion(bf16[2,4096,4096]{2,1,0:T(8,128)(2,1)} %all-gather.5.cloned.1.call-done, bf16[2,4096,2048]{2,1,0:T(8,128)(2,1)} %param.20), kind=kOutput, calls=%fused_computation.143 | convolution fusion | flops 137438953472 | bytes 150994944 | tf_op jit(solution)/shard_map/btd,df->btf/dot_general | solution.py:72
  2691.4 166.7 %fusion.16 = bf16[2,4096,4096]{2,1,0:T(8,128)(2,1)} fusion(f32[2,4096,4096,1]{2,1,3,0:T(8,128)} %fusion.198, f32[2,4096,2048]{2,1,0:T(8,128)} %fusion.81, f32[2048]{0:T(1024)S(1)} %bitcast.206, bf16[2,2048,4096]{2,1,0:T(8,128)(2,1)} %param.22), kind=kOutput, calls=%fused_computation.17 | convolution fusion | flops 137673834496 | bytes 285220864 | tf_op jit(solution)/shard_map/btf,fd->btd/dot_general | solution.py:73
  2861.8 8.2 slice_bitcast_fusion
  2874.3 8.4 slice_bitcast_fusion.1
  2882.8 11.3 maximum_maximum_fusion
  2894.1 21.2 copy.53
  2915.2 13.8 pad_maximum_fusion.2
  2929.0 303.9 %reduce-scatter.5.cloned.1.call-done = bf16[2,512,4096]{2,1,0:T(8,128)(2,1)} async-done(((bf16[2,4096,4096]{2,1,0:T(8,128)(2,1)}), bf16[2,512,4096]{2,1,0:T(8,128)(2,1)}) %reduce-scatter.5.cloned.1.call-update) | async-done | bytes 8388624 | tf_op jit(solution)/shard_map/reduce_scatter | solution.py:75
  3233.0 10.7 fusion.79
  (242 shorter events, 292.2 us)
Async XLA Ops:
  7.2 315.4 %all-gather.3.cloned.1.call-start = ((), (), s32[]{:S(2)}) async-start(), calls=%async_computation.2 | async-start | bytes 75497472 | tf_op jit(solution)/shard_map/all_gather | solution.py:66
  7.2 5.8 copy-start.4
  7.2 8.1 copy-start.33
  7.2 8.7 copy-start.34
  22.4 1598.4 %reduce-scatter.3.cloned.1.call-start = ((), (), s32[]{:S(2)}) async-start(), calls=%async_computation.3 | async-start | bytes 75497472 | tf_op jit(solution)/shard_map/reduce_scatter | solution.py:75
  50.6 11.4 copy-start.32
  50.6 14.9 copy-start.36
  79.7 13.9 slice-start.10
  85.7 8.0 slice-start.11
  429.0 14.0 copy-start.9
  429.0 14.0 copy-start.11
  455.1 15.9 copy-start.6
  476.7 8.8 slice-start.2
  480.9 4.6 slice-start.3
  480.9 4.6 copy-start.1
  480.9 5.6 copy-start.2
  480.9 11.7 slice-start.6
  486.6 6.0 slice-start.7
  538.8 19.4 copy-start.27
  558.3 8.1 copy-start.25
  566.3 13.6 copy-start.23
  579.9 16.7 copy-start.21
  596.6 21.0 copy-start.19
  617.7 25.6 copy-start.17
  750.3 41.9 %copy-start.40 = (f32[2,2,512]{2,1,0:T(2,128)S(1)}, f32[2,2,512]{2,1,0:T(2,128)}, u32[]{:S(2)}) copy-start(f32[2,2,512]{2,1,0:T(2,128)} %get-tuple-element.32) | copy-start | bytes 24580
  792.1 12.9 copy-start.13
  792.1 7.2 copy-start.42
  799.3 5.7 copy-start.44
  805.0 7.5 copy-start.46
  812.5 10.3 copy-start.48
  822.9 11.2 copy-start.14
  822.9 11.2 copy-start.50
  834.1 11.1 copy-start.52
  845.1 14.6 copy-start.54
  927.9 151.4 %copy-start.38 = (f32[1,2048]{1,0:T(1,128)S(1)}, f32[1,2048]{1,0:T(1,128)}, u32[]{:S(2)}) copy-start(f32[1,2048]{1,0:T(1,128)} %get-tuple-element.31) | copy-start | bytes 24580
  1245.9 689.0 %all-gather.5.cloned.1.call-start = ((), (), s32[]{:S(2)}) async-start(), calls=%async_computation.4 | async-start | bytes 75497472 | tf_op jit(solution)/shard_map/all_gather | solution.py:66
  1637.5 1595.4 %reduce-scatter.5.cloned.1.call-start = ((), (), s32[]{:S(2)}) async-start(), calls=%async_computation.5 | async-start | bytes 75497472 | tf_op jit(solution)/shard_map/reduce_scatter | solution.py:75
  2041.3 14.1 copy-start.10
  2041.3 14.1 copy-start.12
  2067.5 15.8 copy-start.8
  2089.0 8.9 slice-start
  2093.3 5.6 copy-start.3
  2093.3 11.5 slice-start.4
  2098.9 5.9 slice-start.5
  2151.0 19.4 copy-start.28
  2170.4 8.0 copy-start.26
  2178.4 13.6 copy-start.24
  2192.1 16.7 copy-start.22
  2208.8 21.0 copy-start.20
  2229.8 25.5 copy-start.18
  2362.4 41.9 %copy-start.39 = (f32[2,2,512]{2,1,0:T(2,128)S(1)}, f32[2,2,512]{2,1,0:T(2,128)}, u32[]{:S(2)}) copy-start(f32[2,2,512]{2,1,0:T(2,128)} %get-tuple-element.48) | copy-start | bytes 24580
  2404.2 12.9 copy-start.15
  2404.3 7.2 copy-start.41
  2411.4 5.7 copy-start.43
  2417.2 7.5 copy-start.45
  2424.7 10.3 copy-start.47
  2435.0 11.2 copy-start.16
  2435.0 11.2 copy-start.49
  2446.2 11.1 copy-start.51
  2457.3 14.6 copy-start.53
  2540.0 151.4 %copy-start.37 = (f32[1,2048]{1,0:T(1,128)S(1)}, f32[1,2048]{1,0:T(1,128)}, u32[]{:S(2)}) copy-start(f32[1,2048]{1,0:T(1,128)} %get-tuple-element.30) | copy-start | bytes 24580
  2870.1 12.7 slice-start.8
  2874.3 8.4 slice-start.9
  2915.2 317.7 %copy-start.31 = (f32[1,4096]{1,0:T(1,128)S(1)}, f32[1,4096]{1,0:T(1,128)}, u32[]{:S(2)}) copy-start(f32[1,4096]{1,0:T(1,128)} %get-tuple-element.22) | copy-start | bytes 49156
  (7 other events, 21.7 us)
Sparse Core Ops, SparseCore 0:
  22.5 300.0 all-gather.2
  1246.0 374.6 reduce-scatter.2
  1637.7 297.2 all-gather.4
  2858.2 374.7 reduce-scatter.4
where the time goes:
time: 3260 us; the launch traced here: 3250 us
  matrix products  1320 us (40%)
  waiting for transfers between devices  1170 us (36%)
  other arithmetic  529 us (16%)
  local copies, waits for them, and re-layouts  211 us (6%)
    reduce_scatter x2, waiting for transfers between devices, device_step(): lax.psum_scatter(branch_sum, 'tp', scatter_dimension=1, tiled=True)  677 us
    all_gather x2, waiting for transfers between devices, device_step(): gathered = lax.all_gather(normed, 'tp', axis=1, tiled=True)  496 us
    sub x16, other arithmetic, causal_attention(): attn_probs = jax.nn.softmax(scores, axis=-1).astype(jnp.bfloat16)  384 us
    dot_general x2, matrix products, device_step(): jnp.einsum('btf,fd->btd', fc_hidden, w_fc_out[layer_idx], preferred_eleme...  333 us
    dot_general x2, matrix products, device_step(): jnp.einsum('btd,df->btf', gathered, w_fc_in[layer_idx], preferred_element...  303 us
    dot_general x16, matrix products, causal_attention(): jnp.einsum('bhqk,bhke->bhqe', attn_probs, values_all[:, :, :stop_at], pre...  168 us
    dot_general x16, matrix products, causal_attention(): jnp.einsum('bhqe,bhke->bhqk', query_all[:, :, start_at:stop_at], keys_all...  152 us
    dot_general x2, matrix products, device_step(): jnp.einsum('bhte,hed->btd', context, w_attn_out[layer_idx], preferred_ele...  103 us
  transfers between devices with their start and end apart: 4, of which 4 were waited for; matrix products, arithmetic and copies ran while one was open for 5% of the time, Pallas kernels for 0%

commit v1 on v0

v1 whole, which is shorter than its diff:
```python
import functools

import jax
import jax.numpy as jnp
from jax import lax
from jax.experimental import pallas as pl
from jax.experimental.pallas import tpu as pltpu
from jax.sharding import Mesh, PartitionSpec as P


ROTARY_DIM = 64
LN_EPS = 1e-5
LANES = 128
PIECES = 2
LOG2E = 1.4426950408889634
MASKED = -1e30


def layer_norm(hidden_rows, gain_vec, bias_vec):
    rows_f32 = hidden_rows.astype(jnp.float32)
    row_mean = jnp.mean(rows_f32, axis=-1, keepdims=True)
    centered = rows_f32 - row_mean
    row_var = jnp.mean(centered * centered, axis=-1, keepdims=True)
    return (centered * lax.rsqrt(row_var + LN_EPS) * gain_vec + bias_vec).astype(jnp.bfloat16)


def norm_body(has_partial, waits, *refs):
    inputs = 5 if has_partial else 3
    refs = refs[:inputs] + refs[inputs + waits :]
    if has_partial:
        held_ref, part_ref, shift_ref, gain_ref, bias_ref, new_ref, normed_ref = refs
        rows = held_ref[...].astype(jnp.float32) + part_ref[...].astype(jnp.float32) + shift_ref[...]
        new_ref[...] = rows.astype(new_ref.dtype)
        rows = new_ref[...]
    else:
        held_ref, gain_ref, bias_ref, normed_ref = refs
        rows = held_ref[...]
    normed_ref[...] = layer_norm(rows, gain_ref[...], bias_ref[...])


def residual_norm(held, gain, bias, partial=None, shift=None, after=()):
    rows, d = held.shape
    block = min(rows, 128)
    row_spec = pl.BlockSpec((block, d), lambda i: (i, 0))
    vec_spec = pl.BlockSpec((1, d), lambda i: (0, 0))
    out = jax.ShapeDtypeStruct((rows, d), jnp.bfloat16)
    vec = lambda a: a.reshape(1, d)
    has_partial = partial is not None
    operands = [held] + ([partial, vec(shift)] if has_partial else []) + [vec(gain), vec(bias), *after]
    specs = [row_spec] + ([row_spec, vec_spec] if has_partial else []) + [vec_spec] * 2 + [pl.BlockSpec(memory_space=pl.ANY)] * len(after)
    return pl.pallas_call(
        functools.partial(norm_body, has_partial, len(after)),
        grid=(rows // block,),
        in_specs=specs,
        out_specs=[row_spec] * (1 + has_partial),
        out_shape=[out] * (1 + has_partial),
        name="residual_norm",
        cost_estimate=pl.CostEstimate(flops=12 * rows * d, bytes_accessed=8 * rows * d, transcendentals=0),
    )(*operands)


def rotary_lanes(seq_full):
    positions = jnp.arange(seq_full).astype(jnp.float32)
    inv_freq = 10000.0 ** (-jnp.arange(0, ROTARY_DIM, 2).astype(jnp.float32) / ROTARY_DIM)
    angles = positions[:, None] * jnp.repeat(inv_freq, 2)[None, :]
    rest = ((0, 0), (0, LANES - ROTARY_DIM))
    cos_tab = jnp.pad(jnp.cos(angles), rest, constant_values=1.0)
    sin_tab = jnp.pad(jnp.sin(angles), rest)
    even = (jnp.arange(LANES) % 2 == 0)[None, :]
    return cos_tab, jnp.where(even, -sin_tab, 0.0), jnp.where(even, 0.0, sin_tab)


def qkv_body(heads, head_dim, *refs):
    pieces = refs[:-9]
    wq_ref, wk_ref, wv_ref, cos_ref, up_ref, down_ref, q_ref, k_ref, v_ref = refs[-9:]
    rows = jnp.concatenate([piece[...] for piece in pieces], axis=0)
    for w_ref, o_ref, turned in ((wq_ref, q_ref, True), (wk_ref, k_ref, True), (wv_ref, v_ref, False)):
        projected = jnp.dot(rows, w_ref[...], preferred_element_type=jnp.float32)
        for head in range(heads):
            lo = head * head_dim
            if turned:
                first = projected[:, lo : lo + LANES]
                first = first * cos_ref[...] + pltpu.roll(first, LANES - 1, 1) * up_ref[...] + pltpu.roll(first, 1, 1) * down_ref[...]
                o_ref[head, :, :LANES] = first.astype(o_ref.dtype)
                o_ref[head, :, LANES:] = projected[:, lo + LANES : lo + head_dim].astype(o_ref.dtype)
            else:
                o_ref[head] = projected[:, lo : lo + head_dim].astype(o_ref.dtype)


def project_qkv(pieces, wq, wk, wv, tables, layer, heads, head_dim):
    devices, rows, d = pieces[0].shape
    block = rows * len(pieces)
    width = heads * head_dim
    weight_spec = pl.BlockSpec((None, d, width), lambda i: (layer, 0, 0), pipeline_mode=pl.Buffered(1))
    table_spec = pl.BlockSpec((block, LANES), lambda i: (i, 0))
    out_spec = pl.BlockSpec((heads, block, head_dim), lambda i: (0, i, 0))
    out = jax.ShapeDtypeStruct((heads, devices * block, head_dim), jnp.bfloat16)
    return pl.pallas_call(
        functools.partial(qkv_body, heads, head_dim),
        grid=(devices,),
        in_specs=[pl.BlockSpec((None, rows, d), lambda i: (i, 0, 0))] * len(pieces) + [weight_spec] * 3 + [table_spec] * 3,
        out_specs=[out_spec] * 3,
        out_shape=[out] * 3,
        name="project_qkv",
        cost_estimate=pl.CostEstimate(flops=6 * devices * block * d * width, bytes_accessed=2 * devices * block * d + 6 * d * width + 6 * devices * block * width, transcendentals=0),
        compiler_params=pltpu.CompilerParams(dimension_semantics=("arbitrary",), vmem_limit_bytes=60 * 1024 * 1024),
    )(*pieces, wq, wk, wv, *tables)


def attention_body(heads, head_dim, block, batch_idx, lengths_ref, q_ref, k_ref, v_ref, *rest):
    o_ref = rest[-1]
    length = lengths_ref[batch_idx]
    q_idx = pl.program_id(0)
    whole = jnp.minimum(q_idx, length // block)
    scale = LOG2E * head_dim**-0.5

    def scores_of(head, k_idx):
        keys = k_ref[head, pl.ds(pl.multiple_of(k_idx * block, block), block), :]
        return lax.dot_general(q_ref[head], keys, (((1,), (1,)), ((), ())), preferred_element_type=jnp.float32) * scale

    def values_of(head, k_idx):
        return v_ref[head, pl.ds(pl.multiple_of(k_idx * block, block), block), :]

    q_pos = q_idx * block + lax.broadcasted_iota(jnp.int32, (block, block), 0)
    k_pos = whole * block + lax.broadcasted_iota(jnp.int32, (block, block), 1)
    allowed = (k_pos <= q_pos) & (k_pos < length)
    state = []
    for head in range(heads):
        scores = jnp.where(allowed, scores_of(head, whole), MASKED)
        top = jnp.max(scores, axis=1, keepdims=True)
        probs = jnp.exp2(scores - top)
        total = jnp.sum(probs, axis=1, keepdims=True)
        acc = jnp.dot(probs.astype(jnp.bfloat16), values_of(head, whole), preferred_element_type=jnp.float32)
        state.append((top, total, acc))

    def step(k_idx, state):
        out = []
        for head, (top, total, acc) in enumerate(state):
            scores = scores_of(head, k_idx)
            new_top = jnp.maximum(top, jnp.max(scores, axis=1, keepdims=True))
            probs = jnp.exp2(scores - new_top)
            shrink = jnp.exp2(top - new_top)
            total = total * shrink + jnp.sum(probs, axis=1, keepdims=True)
            acc = acc * shrink + jnp.dot(probs.astype(jnp.bfloat16), values_of(head, k_idx), preferred_element_type=jnp.float32)
            out.append((new_top, total, acc))
        return tuple(out)

    state = lax.fori_loop(0, whole, step, tuple(state))
    for head, (_, total, acc) in enumerate(state):
        o_ref[:, head * head_dim : (head + 1) * head_dim] = (acc / total).astype(o_ref.dtype)


def causal_attention(lengths, query_all, keys_all, values_all, batch_idx, block, after=()):
    heads, seq, head_dim = query_all.shape
    whole_spec = pl.BlockSpec((heads, seq, head_dim), lambda i, *_: (0, 0, 0))
    return pl.pallas_call(
        functools.partial(attention_body, heads, head_dim, block, batch_idx),
        grid_spec=pltpu.PrefetchScalarGridSpec(
            num_scalar_prefetch=1,
            grid=(seq // block,),
            in_specs=[pl.BlockSpec((heads, block, head_dim), lambda i, *_: (0, i, 0)), whole_spec, whole_spec] + [pl.BlockSpec(memory_space=pl.ANY)] * len(after),
            out_specs=pl.BlockSpec((block, heads * head_dim), lambda i, *_: (i, 0)),
        ),
        out_shape=jax.ShapeDtypeStruct((seq, heads * head_dim), jnp.bfloat16),
        name="causal_attention",
        cost_estimate=pl.CostEstimate(flops=4 * heads * seq * seq * head_dim, bytes_accessed=8 * heads * seq * head_dim, transcendentals=heads * seq * seq // 2),
        compiler_params=pltpu.CompilerParams(dimension_semantics=("arbitrary",), vmem_limit_bytes=60 * 1024 * 1024),
    )(lengths, query_all, keys_all, values_all, *after)


def out_body(ctx_ref, fc_ref, wo_ref, w_ref, o_ref, send_ref, recv_ref, send_sem, recv_sem):
    n, h, side = (pl.program_id(i) for i in range(3))
    halves = pl.num_programs(1)
    sibling = 1 - lax.axis_index("core")
    slot = n * halves + h

    def exchange():
        return pltpu.make_async_remote_copy(
            src_ref=send_ref, dst_ref=recv_ref.at[slot], send_sem=send_sem, recv_sem=recv_sem.at[slot], device_id={"core": sibling}, device_id_type=pl.DeviceIdType.MESH
        )

    @pl.when((n == 0) & (h == 0) & (side == 0))
    def _():
        barrier = pltpu.get_barrier_semaphore()
        pl.semaphore_signal(barrier, inc=1, device_id={"core": sibling}, device_id_type=pl.DeviceIdType.MESH)
        pl.semaphore_wait(barrier, 1)

    @pl.when(side == 1)
    def _():
        exchange().start()

    groups, rows, width = ctx_ref.shape
    total = jnp.dot(fc_ref[...].reshape(groups * rows, fc_ref.shape[-1]), w_ref[...], preferred_element_type=jnp.float32)
    total += jnp.dot(ctx_ref[...].reshape(groups * rows, width), wo_ref[...], preferred_element_type=jnp.float32)

    @pl.when(side == 0)
    def _():
        send_ref[...] = total.astype(send_ref.dtype)

    @pl.when(side == 1)
    def _():
        exchange().wait()
        o_ref[...] = (total + recv_ref[slot].astype(jnp.float32)).astype(o_ref.dtype).reshape(o_ref.shape)


def project_out(context, fc_hidden, wo, w_out, layer, piece, collective_id):
    chips, cores, _, rows, width = context.shape
    ff = fc_hidden.shape[-1]
    d = wo.shape[-1]
    group = min(chips, max(1, 1024 // rows))
    cols = 1024
    halves = chips // group
    block = group * rows

    def core_of(side):
        return lax.rem(lax.axis_index("core") + 1 + side, 2)

    work = chips * cores * rows
    return pl.pallas_call(
        out_body,
        grid=(d // cols, halves, cores),
        in_specs=[
            pl.BlockSpec((group, None, None, rows, width), lambda n, h, s: (h, core_of(s), piece, 0, 0)),
            pl.BlockSpec((group, None, None, rows, ff), lambda n, h, s: (h, core_of(s), 0, 0, 0)),
            pl.BlockSpec((None, width, cols), lambda n, h, s: (layer, 0, n)),
            pl.BlockSpec((None, ff, cols), lambda n, h, s: (layer, 0, n)),
        ],
        out_specs=pl.BlockSpec((group, rows, cols), lambda n, h, s: (h, 0, n)),
        out_shape=jax.ShapeDtypeStruct((chips, rows, d), jnp.bfloat16),
        scratch_shapes=[
            pltpu.VMEM((block, cols), jnp.bfloat16),
            pltpu.VMEM((d // cols * halves, block, cols), jnp.bfloat16),
            pltpu.SemaphoreType.DMA,
            pltpu.SemaphoreType.DMA((d // cols * halves,)),
        ],
        name="project_out",
        cost_estimate=pl.CostEstimate(flops=2 * work * (ff + width) * d, bytes_accessed=2 * (work * (ff + width + d) + (ff + width) * d), transcendentals=0),
        compiler_params=pltpu.CompilerParams(dimension_semantics=("arbitrary",) * 3, vmem_limit_bytes=63 * 1024 * 1024, collective_id=collective_id, has_side_effects=True),
    )(context, fc_hidden, wo, w_out)


def solution(mesh):
    tp_size = mesh.shape["tp"]
    mesh = Mesh(mesh.devices.reshape(mesh.shape["dp"], tp_size // 2, 2), ("dp", "chip", "core"))
    tp = ("chip", "core")

    def device_step(hidden, lengths, ln_gain, ln_bias, w_query, w_key, w_value, w_attn_out, w_fc_in, b_fc_in, w_fc_out, b_fc_out):
        batch, rows_own, d = hidden.shape
        layers, _, heads, head_dim = w_query.shape
        seq_full = rows_own * tp_size
        tables = rotary_lanes(seq_full)
        wq, wk, wv = (w.reshape(layers, d, heads * head_dim) for w in (w_query, w_key, w_value))
        wo = w_attn_out.reshape(layers, heads * head_dim, d)
        chips = tp_size // 2

        def pieces_of(layer, b):
            return PIECES if (layer, b) in ((0, 0), (layers - 1, batch - 1)) else 1

        def gather(normed, layer, b):
            count = pieces_of(layer, b)
            rows = rows_own // count
            gathered = []
            for piece in range(count):
                gathered.append(lax.all_gather(normed[piece * rows : (piece + 1) * rows], tp, axis=0))
            return gathered

        def fc_in(rows, layer):
            return jax.nn.gelu(jnp.einsum("ntd,df->ntf", rows, w_fc_in[layer], preferred_element_type=jnp.float32) + b_fc_in[layer], approximate=True).astype(jnp.bfloat16)

        held = [hidden[b] for b in range(batch)]
        normed = [residual_norm(held[b], ln_gain[0], ln_bias[0])[0] for b in range(batch)]
        gathered = [gather(normed[b], 0, b) for b in range(batch)]
        cache_k = []
        cache_v = []
        waiting = None
        for layer, b in [(layer, b) for layer in range(layers) for b in range(batch)]:
            pieces = pieces_of(layer, b)
            rows = rows_own // pieces
            first_fc = fc_in(gathered[b][0], layer)
            query_all, keys_all, values_all = project_qkv(gathered[b], wq, wk, wv, tables, layer, heads, head_dim)
            cache_k.append(keys_all)
            cache_v.append(values_all)
            after = [first_fc]
            if waiting is not None and waiting[0] < layers - 1:
                up, prompt, sums = waiting
                held[prompt], normed[prompt] = residual_norm(held[prompt], ln_gain[up + 1], ln_bias[up + 1], sums, b_fc_out[up], [first_fc, query_all])
                gathered[prompt] = gather(normed[prompt], up + 1, prompt)
                after.append(normed[prompt])
            elif waiting is not None:
                held[waiting[1]] = (held[waiting[1]].astype(jnp.float32) + waiting[2].astype(jnp.float32) + b_fc_out[layer]).astype(jnp.bfloat16)
            context = causal_attention(lengths, query_all, keys_all, values_all, b, rows_own, after)
            context = context.reshape(chips, 2, pieces, rows, heads * head_dim)
            reduced = []
            part = None
            for piece in range(pieces):
                if piece == 0:
                    fc = first_fc
                else:
                    source, _ = lax.optimization_barrier((gathered[b][piece], part))
                    fc = fc_in(source, layer)
                fc = fc.reshape(chips, 2, 1, rows, -1)
                part = project_out(context, fc, wo, w_fc_out, layer, piece, (layer * batch + b) * PIECES + piece)
                reduced.append(lax.psum_scatter(part, "chip", scatter_dimension=0))
            waiting = (layer, b, jnp.concatenate(reduced, axis=0))
        layer, b, sums = waiting
        held[b] = (held[b].astype(jnp.float32) + sums.astype(jnp.float32) + b_fc_out[layer]).astype(jnp.bfloat16)
        cache_shape = (layers, batch, heads, seq_full, head_dim)
        return jnp.stack(held), jnp.stack(cache_k).reshape(cache_shape), jnp.stack(cache_v).reshape(cache_shape)

    head_cols = P(None, None, tp, None)
    cache_spec = P(None, "dp", tp, None, None)
    hidden_spec = P("dp", tp, None)
    return jax.shard_map(device_step, mesh=mesh, in_specs=(hidden_spec, P("dp"), P(), P(), head_cols, head_cols, head_cols, P(None, tp, None, None), P(None, None, tp), P(None, tp), P(None, tp, None), P()), out_specs=(hidden_spec, cache_spec, cache_spec), check_vma=False)
```

time: 3260 us -> 1910 us (0.59)
  matrix products: 1320 us -> 353 us
  Pallas kernels: 0 us -> 844 us
  waiting for transfers between devices: 1170 us -> 574 us
  other arithmetic: 529 us -> 54.2 us
  local copies, waits for them, and re-layouts: 211 us -> 61.8 us
    dot_general x44 -> x6, matrix products: 1320 us -> 353 us  [fc_in(): jnp.einsum('ntd,df->ntf', rows, w_fc_in[layer], preferred_element_type=jn...]
    pallas_call x0 -> x18, Pallas kernels: none -> 844 us  [the longest x6 417 us: project_out(): pl.pallas_call(out_body, grid=(d // cols, halves, cores), in_specs=[pl.Bl...]
    reduce_scatter x2 -> x0, waiting for transfers between devices: 677 us -> none  [device_step(): lax.psum_scatter(branch_sum, 'tp', scatter_dimension=1, tiled=True)]
    sub x18 -> x0, other arithmetic: 398 us -> none  [the longest x16 384 us: causal_attention(): attn_probs = jax.nn.softmax(scores, axis=-1).astype(jnp.bfloat16)]
    unnamed x4 -> x18, waiting for transfers between devices: 0.07 us -> 303 us
    all_gather x2 -> x6, waiting for transfers between devices: 496 us -> 271 us  [gather(): lax.all_gather(normed[piece * rows:(piece + 1) * rows], tp, axis=0)]
    unnamed x139 -> x22, local copies, waits for them, and re-layouts: 73.1 us -> 0.05 us
    slice x15 -> x5, local copies, waits for them, and re-layouts: 77.6 us -> 11.3 us  [the longest x2 9.41 us: gather(): normed[piece * rows:(piece + 1) * rows]]
  transfers between devices with their start and end apart: 4 -> 12, of which waited for: 4 -> 10; matrix products, arithmetic and copies ran while one was open for 5% -> 16% of each run, Pallas kernels for 0% -> 28%
where the time goes in v1:
time: 1910 us; the launch traced here: 1900 us
  Pallas kernels  844 us (44%)
  waiting for transfers between devices  574 us (30%)
  matrix products  353 us (18%)
  local copies, waits for them, and re-layouts  61.8 us (3%)
  other arithmetic  54.2 us (3%)
    pallas_call x6, Pallas kernels, project_out(): pl.pallas_call(out_body, grid=(d // cols, halves, cores), in_specs=[pl.Bl...  417 us
    dot_general x6, matrix products, fc_in(): jnp.einsum('ntd,df->ntf', rows, w_fc_in[layer], preferred_element_type=jn...  353 us
    unnamed x18, waiting for transfers between devices  303 us
    all_gather x6, waiting for transfers between devices, gather(): lax.all_gather(normed[piece * rows:(piece + 1) * rows], tp, axis=0)  271 us
    pallas_call x4, Pallas kernels, project_qkv(): pl.pallas_call(functools.partial(qkv_body, heads, head_dim), grid=(device...  247 us
    pallas_call x4, Pallas kernels, causal_attention(): pl.pallas_call(functools.partial(attention_body, heads, head_dim, block,...  147 us
    reshape x3, local copies, waits for them, and re-layouts, device_step(): w.reshape(layers, d, heads * head_dim)  42.8 us
  transfers between devices with their start and end apart: 12, of which 10 were waited for; matrix products, arithmetic and copies ran while one was open for 16% of the time, Pallas kernels for 28%

profile of v1, /device:TPU:0, one launch (start us, length us, event | category | flops | bytes accessed | tf_op | source)
XLA Modules:
  0.0 1902.1 jit_solution(13049617301188531055)
XLA Ops:
  7.2 6.0 slice_bitcast_fusion.1
  13.2 0.7 fusion.80
  13.9 7.0 residual_norm.4
  20.9 4.7 fusion.78
  25.7 0.0 all-gather.15.cloned.1.call-start
  25.7 0.7 all-gather.15.cloned.1.call-update
  26.5 0.1 broadcast_in_dim.29
  26.6 0.1 mul.106
  26.7 14.4 reshape.73.refs_2_.refs_1_
  41.0 14.0 reshape.74.refs_3_.refs_2_
  55.1 14.4 reshape.75.refs_4_.refs_3_
  69.5 7.3 multiply_sine_fusion
  76.7 1.5 pad.8.refs_5_.refs_4_
  78.2 0.6 fusion.82
  78.9 2.3 pad_select_fusion
  81.2 31.6 %all-gather.13.cloned.1.call-done = bf16[2048,4096]{1,0:T(8,128)(2,1)} async-done(((bf16[256,4096]{1,0:T(8,128)(2,1)}), bf16[2048,4096]{1,0:T(8,128)(2,1)}) %all-gather.13.cloned.1.call-update) | async-done | bytes 16777232 | tf_op jit(solution)/shard_map/all_gather | solution.py:264
  112.8 46.1 %fusion.23.rest_0_ = bf16[8,256,2048]{2,1,0:T(8,128)(2,1)} fusion(f32[2048]{0:T(1024)S(1)} %bitcast.110, bf16[8,256,4096]{2,1,0:T(8,128)(2,1)} %bitcast.119, bf16[2,4096,2048]{2,1,0:T(8,128)(2,1)} %param.20), kind=kOutput, calls=%fused_computation.29 | convolution fusion | flops 34401681408 | bytes 41951232 | tf_op jit(solution)/shard_map/ntd,df->ntf/dot_general | solution.py:268
  158.9 39.9 %all-gather.15.cloned.1.call-done = bf16[2048,4096]{1,0:T(8,128)(2,1)} async-done(((bf16[256,4096]{1,0:T(8,128)(2,1)}), bf16[2048,4096]{1,0:T(8,128)(2,1)}) %all-gather.15.cloned.1.call-update) | async-done | bytes 16777232 | tf_op jit(solution)/shard_map/all_gather | solution.py:264
  198.8 62.2 %project_qkv.4 = (bf16[2,4096,256]{2,1,0:T(8,128)(2,1)}, bf16[2,4096,256]{2,1,0:T(8,128)(2,1)}, bf16[2,4096,256]{2,1,0:T(8,128)(2,1)}) custom-call(bf16[8,256,4096]{2,1,0:T(8,128)(2,1)} %bitcast.120, bf16[8,256,4096]{2,1,0:T(8,128)(2,1)} %bitcast.121, bf16[2,4096,512]{2,1,0:T(8,128)(2,1)} %reshape.73.refs_2_.refs_1_, ...), custom_call_target="tpu_custom_call" | custom-call | flops 51539607552 | bytes 58720256 | tf_op jit(solution)/shard_map/project_qkv/pallas_call | solution.py:98
  261.0 55.6 %causal_attention.4 = bf16[4096,512]{1,0:T(8,128)(2,1)} custom-call(s32[2]{0:T(128)} %lengths_ref.7, bf16[2,4096,256]{2,1,0:T(8,128)(2,1)} %get-tuple-element.21.q_ref, bf16[2,4096,256]{2,1,0:T(8,128)(2,1)} %get-tuple-element.22.k_ref, bf16[2,4096,256]{2,1,0:T(8,128)(2,1)} %get-tuple-element.23.v_ref, bf16[8,256,2048]{2,1,0:T(8,128)(2,1)} %fusion.23.rest_0_), custom_call_target="tpu_custom_call" | custom-call | flops 34359738368 | bytes 16777216 | tf_op jit(solution)/shard_map/causal_attention/pallas_call | solution.py:156
  316.6 53.3 %project_out.6 = bf16[4,256,4096]{2,1,0:T(8,128)(2,1)} custom-call(bf16[4,2,2,256,512]{4,3,2,1,0:T(8,128)(2,1)} %bitcast.137, bf16[4,2,1,256,2048]{4,3,2,1,0:T(8,128)(2,1)} %bitcast.131, bf16[2,512,4096]{2,1,0:T(8,128)(2,1)} %bitcast.125, bf16[2,2048,4096]{2,1,0:T(8,128)(2,1)} %w_ref.11), custom_call_target="tpu_custom_call" | custom-call | flops 42949672960 | bytes 48234496 | tf_op jit(solution)/shard_map/project_out/pallas_call | solution.py:219
  370.0 46.0 %fusion.31 = bf16[8,256,2048]{2,1,0:T(8,128)(2,1)} fusion(f32[2048]{0:T(1024)S(1)} %bitcast.111, bf16[8,256,4096]{2,1,0:T(8,128)(2,1)} %bitcast.122, bf16[2,4096,2048]{2,1,0:T(8,128)(2,1)} %param.20), kind=kOutput, calls=%fused_computation.37 | convolution fusion | flops 34401681408 | bytes 41951232 | tf_op jit(solution)/shard_map/ntd,df->ntf/dot_general | solution.py:268
  416.0 53.4 %project_out.7 = bf16[4,256,4096]{2,1,0:T(8,128)(2,1)} custom-call(bf16[4,2,2,256,512]{4,3,2,1,0:T(8,128)(2,1)} %bitcast.138, bf16[4,2,1,256,2048]{4,3,2,1,0:T(8,128)(2,1)} %bitcast.134, bf16[2,512,4096]{2,1,0:T(8,128)(2,1)} %bitcast.126, bf16[2,2048,4096]{2,1,0:T(8,128)(2,1)} %w_ref.11), custom_call_target="tpu_custom_call" | custom-call | flops 42949672960 | bytes 48234496 | tf_op jit(solution)/shard_map/project_out/pallas_call | solution.py:219
  469.4 0.0 reduce-scatter.19.cloned.1.call-start
  469.5 0.5 reduce-scatter.19.cloned.1.call-update
  470.0 7.2 residual_norm.5
  477.2 0.2 all-gather.19.cloned.1.call-start
  477.5 0.6 fusion.79
  478.1 72.2 %reduce-scatter.21.cloned.1.call-done = bf16[1,256,4096]{2,1,0:T(8,128)(2,1)} async-done(((bf16[4,256,4096]{2,1,0:T(8,128)(2,1)}), bf16[1,256,4096]{2,1,0:T(8,128)(2,1)}) %reduce-scatter.21.cloned.1.call-update) | async-done | bytes 2097168
  550.3 83.6 %reduce-scatter.19.cloned.1.call-done = bf16[1,256,4096]{2,1,0:T(8,128)(2,1)} async-done(((bf16[4,256,4096]{2,1,0:T(8,128)(2,1)}), bf16[1,256,4096]{2,1,0:T(8,128)(2,1)}) %reduce-scatter.19.cloned.1.call-update) | async-done | bytes 2097168
  633.9 4.8 pad_maximum_fusion.3.refs_1_
  638.7 152.6 %all-gather.17.cloned.1.call-done = bf16[4096,4096]{1,0:T(8,128)(2,1)} async-done(((bf16[512,4096]{1,0:T(8,128)(2,1)}), bf16[4096,4096]{1,0:T(8,128)(2,1)}) %all-gather.17.cloned.1.call-update) | async-done | bytes 33554448 | tf_op jit(solution)/shard_map/all_gather | solution.py:264
  791.3 60.9 %project_qkv.5 = (bf16[2,4096,256]{2,1,0:T(8,128)(2,1)}, bf16[2,4096,256]{2,1,0:T(8,128)(2,1)}, bf16[2,4096,256]{2,1,0:T(8,128)(2,1)}) custom-call(bf16[8,512,4096]{2,1,0:T(8,128)(2,1)} %bitcast.115, bf16[2,4096,512]{2,1,0:T(8,128)(2,1)} %reshape.73.refs_2_.refs_1_, bf16[2,4096,512]{2,1,0:T(8,128)(2,1)} %reshape.74.refs_3_.refs_2_, ...), custom_call_target="tpu_custom_call" | custom-call | flops 51539607552 | bytes 58720256 | tf_op jit(solution)/shard_map/project_qkv/pallas_call | solution.py:98
  852.2 84.1 %fusion.7.refs_5_.rest_0_ = bf16[8,512,2048]{2,1,0:T(8,128)(2,1)} fusion(bf16[8,512,4096]{2,1,0:T(8,128)(2,1)} %bitcast.116, f32[2048]{0:T(1024)S(1)} %bitcast.112, bf16[2,4096,2048]{2,1,0:T(8,128)(2,1)} %param.20), kind=kOutput, calls=%fused_computation.9 | convolution fusion | flops 68803362816 | bytes 67117056 | tf_op jit(solution)/shard_map/ntd,df->ntf/dot_general | solution.py:268
  936.4 9.2 residual_norm.6
  945.6 0.0 reduce-scatter.23.cloned.1.call-start
  945.6 17.5 causal_attention.5
  963.1 102.6 %project_out.8 = bf16[4,512,4096]{2,1,0:T(8,128)(2,1)} custom-call(bf16[4,2,1,512,512]{4,3,2,1,0:T(8,128)(2,1)} %bitcast.140, bf16[4,2,1,512,2048]{4,3,2,1,0:T(8,128)(2,1)} %bitcast.92, bf16[2,512,4096]{2,1,0:T(8,128)(2,1)} %bitcast.127, bf16[2,2048,4096]{2,1,0:T(8,128)(2,1)} %w_ref.11), custom_call_target="tpu_custom_call" | custom-call | flops 85899345920 | bytes 75497472 | tf_op jit(solution)/shard_map/project_out/pallas_call | solution.py:219
  1065.7 0.0 all-gather.23.cloned.1.call-start
  1065.8 35.1 %all-gather.19.cloned.1.call-done = bf16[4096,4096]{1,0:T(8,128)(2,1)} async-done(((bf16[512,4096]{1,0:T(8,128)(2,1)}), bf16[4096,4096]{1,0:T(8,128)(2,1)}) %all-gather.19.cloned.1.call-update) | async-done | bytes 33554448 | tf_op jit(solution)/shard_map/all_gather | solution.py:264
  1100.8 61.3 %project_qkv.6 = (bf16[2,4096,256]{2,1,0:T(8,128)(2,1)}, bf16[2,4096,256]{2,1,0:T(8,128)(2,1)}, bf16[2,4096,256]{2,1,0:T(8,128)(2,1)}) custom-call(bf16[8,512,4096]{2,1,0:T(8,128)(2,1)} %bitcast.113, bf16[2,4096,512]{2,1,0:T(8,128)(2,1)} %reshape.73.refs_2_.refs_1_, bf16[2,4096,512]{2,1,0:T(8,128)(2,1)} %reshape.74.refs_3_.refs_2_, ...), custom_call_target="tpu_custom_call" | custom-call | flops 51539607552 | bytes 58720256 | tf_op jit(solution)/shard_map/project_qkv/pallas_call | solution.py:98
  1162.2 84.6 %fusion.15.refs_5_.rest_0_ = bf16[8,512,2048]{2,1,0:T(8,128)(2,1)} fusion(bf16[8,512,4096]{2,1,0:T(8,128)(2,1)} %bitcast.114, f32[2048]{0:T(1024)S(1)} %bitcast.107, bf16[2,4096,2048]{2,1,0:T(8,128)(2,1)} %param.20), kind=kOutput, calls=%fused_computation.17 | convolution fusion | flops 68803362816 | bytes 67117056 | tf_op jit(solution)/shard_map/ntd,df->ntf/dot_general | solution.py:268
  1246.8 5.2 reduce-scatter.23.cloned.1.call-done
  1252.1 9.1 residual_norm.7
  1261.2 4.7 fusion.77
  1265.9 0.7 all-gather.21.cloned.1.call-update
  1266.7 56.4 %causal_attention.6 = bf16[4096,512]{1,0:T(8,128)(2,1)} custom-call(s32[2]{0:T(128)} %lengths_ref.7, bf16[2,4096,256]{2,1,0:T(8,128)(2,1)} %get-tuple-element.28.refs_6_.q_ref, bf16[2,4096,256]{2,1,0:T(8,128)(2,1)} %get-tuple-element.29.k_ref, bf16[2,4096,256]{2,1,0:T(8,128)(2,1)} %get-tuple-element.30.v_ref, bf16[8,512,2048]{2,1,0:T(8,128)(2,1)} %fusion.15.refs_5_.rest_0_, ...), custom_call_target="tpu_custom_call" | custom-call | flops 34359738368 | bytes 16777216 | tf_op jit(solution)/shard_map/causal_attention/pallas_call | solution.py:156
  1323.1 101.2 %project_out.9 = bf16[4,512,4096]{2,1,0:T(8,128)(2,1)} custom-call(bf16[4,2,1,512,512]{4,3,2,1,0:T(8,128)(2,1)} %bitcast.139, bf16[4,2,1,512,2048]{4,3,2,1,0:T(8,128)(2,1)} %bitcast.91, bf16[2,512,4096]{2,1,0:T(8,128)(2,1)} %bitcast.128, bf16[2,2048,4096]{2,1,0:T(8,128)(2,1)} %w_ref.11), custom_call_target="tpu_custom_call" | custom-call | flops 85899345920 | bytes 75497472 | tf_op jit(solution)/shard_map/project_out/pallas_call | solution.py:219
  1424.3 0.0 reduce-scatter.29.cloned.1.call-start
  1424.4 11.8 all-gather.21.cloned.1.call-done
  1436.2 62.1 %project_qkv.7 = (bf16[2,4096,256]{2,1,0:T(8,128)(2,1)}, bf16[2,4096,256]{2,1,0:T(8,128)(2,1)}, bf16[2,4096,256]{2,1,0:T(8,128)(2,1)}) custom-call(bf16[8,256,4096]{2,1,0:T(8,128)(2,1)} %bitcast.123, bf16[8,256,4096]{2,1,0:T(8,128)(2,1)} %bitcast.117, bf16[2,4096,512]{2,1,0:T(8,128)(2,1)} %reshape.73.refs_2_.refs_1_, ...), custom_call_target="tpu_custom_call" | custom-call | flops 51539607552 | bytes 58720256 | tf_op jit(solution)/shard_map/project_qkv/pallas_call | solution.py:98
  1498.3 46.2 %fusion.39.rest_0_ = bf16[8,256,2048]{2,1,0:T(8,128)(2,1)} fusion(f32[2048]{0:T(1024)S(1)} %bitcast.108, bf16[8,256,4096]{2,1,0:T(8,128)(2,1)} %bitcast.124, bf16[2,4096,2048]{2,1,0:T(8,128)(2,1)} %param.20), kind=kOutput, calls=%fused_computation.45 | convolution fusion | flops 34401681408 | bytes 41951232 | tf_op jit(solution)/shard_map/ntd,df->ntf/dot_general | solution.py:268
  1544.5 17.6 causal_attention.7
  1562.1 53.4 %project_out.10 = bf16[4,256,4096]{2,1,0:T(8,128)(2,1)} custom-call(bf16[4,2,2,256,512]{4,3,2,1,0:T(8,128)(2,1)} %bitcast.135, bf16[4,2,1,256,2048]{4,3,2,1,0:T(8,128)(2,1)} %bitcast.132, bf16[2,512,4096]{2,1,0:T(8,128)(2,1)} %bitcast.129, bf16[2,2048,4096]{2,1,0:T(8,128)(2,1)} %w_ref.11), custom_call_target="tpu_custom_call" | custom-call | flops 42949672960 | bytes 48234496 | tf_op jit(solution)/shard_map/project_out/pallas_call | solution.py:219
  1615.6 45.8 %fusion.47 = bf16[8,256,2048]{2,1,0:T(8,128)(2,1)} fusion(f32[2048]{0:T(1024)S(1)} %bitcast.109, bf16[8,256,4096]{2,1,0:T(8,128)(2,1)} %bitcast.118, bf16[2,4096,2048]{2,1,0:T(8,128)(2,1)} %param.20), kind=kOutput, calls=%fused_computation.53 | convolution fusion | flops 34401681408 | bytes 41951232 | tf_op jit(solution)/shard_map/ntd,df->ntf/dot_general | solution.py:268
  1661.4 53.5 %project_out.11 = bf16[4,256,4096]{2,1,0:T(8,128)(2,1)} custom-call(bf16[4,2,2,256,512]{4,3,2,1,0:T(8,128)(2,1)} %bitcast.136, bf16[4,2,1,256,2048]{4,3,2,1,0:T(8,128)(2,1)} %bitcast.133, bf16[2,512,4096]{2,1,0:T(8,128)(2,1)} %bitcast.130, bf16[2,2048,4096]{2,1,0:T(8,128)(2,1)} %w_ref.11), custom_call_target="tpu_custom_call" | custom-call | flops 42949672960 | bytes 48234496 | tf_op jit(solution)/shard_map/project_out/pallas_call | solution.py:219
  1714.9 0.0 reduce-scatter.27.cloned.1.call-start
  1715.0 0.5 reduce-scatter.27.cloned.1.call-update
  1715.6 17.0 pad_maximum_fusion
  1732.6 7.0 pad_maximum_fusion.1
  1739.7 55.9 %reduce-scatter.29.cloned.1.call-done = bf16[1,256,4096]{2,1,0:T(8,128)(2,1)} async-done(((bf16[4,256,4096]{2,1,0:T(8,128)(2,1)}), bf16[1,256,4096]{2,1,0:T(8,128)(2,1)}) %reduce-scatter.29.cloned.1.call-update) | async-done | bytes 2097168
  1795.6 83.6 %reduce-scatter.27.cloned.1.call-done = bf16[1,256,4096]{2,1,0:T(8,128)(2,1)} async-done(((bf16[4,256,4096]{2,1,0:T(8,128)(2,1)}), bf16[1,256,4096]{2,1,0:T(8,128)(2,1)}) %reduce-scatter.27.cloned.1.call-update) | async-done | bytes 2097168
  1879.3 9.4 fusion.67
  1888.7 6.3 pad_maximum_fusion.2
  (40 shorter events, 0.4 us)
Async XLA Ops:
  7.2 6.0 copy-start.6
  7.2 6.0 copy-start.7
  7.2 105.6 %all-gather.13.cloned.1.call-start = ((), (), s32[]{:S(2)}) async-start(), calls=%async_computation.6 | async-start | bytes 18874368 | tf_op jit(solution)/shard_map/all_gather | solution.py:264
  25.7 173.1 %all-gather.15.cloned.1.call-start = ((), (), s32[]{:S(2)}) async-start(), calls=%async_computation.7 | async-start | bytes 18874368 | tf_op jit(solution)/shard_map/all_gather | solution.py:264
  26.4 523.9 %reduce-scatter.21.cloned.1.call-start = ((), (), s32[]{:S(2)}) async-start(), calls=%async_computation.13 | async-start | bytes 10485760
  55.1 23.2 %copy-start.8 = (f32[2,2048]{1,0:T(2,128)S(1)}, f32[2,2048]{1,0:T(2,128)}, u32[]{:S(2)}) copy-start(f32[2,2048]{1,0:T(2,128)} %param.21) | copy-start | bytes 49156
  469.4 8.1 copy-start.5
  469.4 164.5 %reduce-scatter.19.cloned.1.call-start = ((), (), s32[]{:S(2)}) async-start(), calls=%async_computation.12 | async-start | bytes 10485760
  470.0 321.3 %all-gather.17.cloned.1.call-start = ((), (), s32[]{:S(2)}) async-start(), calls=%async_computation.8 | async-start | bytes 37748736 | tf_op jit(solution)/shard_map/all_gather | solution.py:264
  477.2 623.6 %all-gather.19.cloned.1.call-start = ((), (), s32[]{:S(2)}) async-start(), calls=%async_computation.9 | async-start | bytes 37748736 | tf_op jit(solution)/shard_map/all_gather | solution.py:264
  945.6 306.5 %reduce-scatter.23.cloned.1.call-start = ((), (), s32[]{:S(2)}) async-start(), calls=%async_computation.14 | async-start | bytes 20971520
  1065.7 358.7 %all-gather.23.cloned.1.call-start = ((), (), s32[]{:S(2)}) async-start(), calls=%async_computation.11 | async-start | bytes 18874368 | tf_op jit(solution)/shard_map/all_gather | solution.py:264
  1100.8 61.3 %copy-start.9 = (f32[1,2048]{1,0:T(1,128)S(1)}, f32[1,2048]{1,0:T(1,128)}, u32[]{:S(2)}) copy-start(f32[1,2048]{1,0:T(1,128)} %get-tuple-element.57) | copy-start | bytes 24580
  1265.9 170.4 %all-gather.21.cloned.1.call-start = ((), (), s32[]{:S(2)}) async-start(), calls=%async_computation.10 | async-start | bytes 18874368 | tf_op jit(solution)/shard_map/all_gather | solution.py:264
  1266.6 473.1 %reduce-scatter.25.cloned.1.call-start = ((), (), s32[]{:S(2)}) async-start(), calls=%async_computation.15 | async-start | bytes 20971520
  1424.3 371.3 %reduce-scatter.29.cloned.1.call-start = ((), (), s32[]{:S(2)}) async-start(), calls=%async_computation.17 | async-start | bytes 10485760
  1436.2 62.1 %copy-start.10 = (f32[1,2048]{1,0:T(1,128)S(1)}, f32[1,2048]{1,0:T(1,128)}, u32[]{:S(2)}) copy-start(f32[1,2048]{1,0:T(1,128)} %get-tuple-element.57) | copy-start | bytes 24580
  1714.9 164.3 %reduce-scatter.27.cloned.1.call-start = ((), (), s32[]{:S(2)}) async-start(), calls=%async_computation.16 | async-start | bytes 10485760
  1715.5 17.1 copy-start
  1715.5 17.1 copy-start.1
  1715.5 17.1 copy-start.2
  1715.5 17.1 copy-start.3
  1732.6 146.6 %copy-start.4 = (f32[1,4096]{1,0:T(1,128)S(1)}, f32[1,4096]{1,0:T(1,128)}, u32[]{:S(2)}) copy-start(f32[1,4096]{1,0:T(1,128)} %get-tuple-element.47) | copy-start | bytes 49156
Sparse Core Ops, SparseCore 0:
  25.8 86.9 all-gather.12
  114.6 84.1 all-gather.14
  469.5 80.7 reduce-scatter.20
  553.2 80.7 reduce-scatter.18
  636.2 155.0 all-gather.16
  945.7 155.0 all-gather.18
  1103.8 148.1 reduce-scatter.22
  1266.0 84.6 all-gather.22
  1352.5 83.7 all-gather.20
  1439.1 148.1 reduce-scatter.24
  1715.1 80.5 reduce-scatter.28
  1798.5 80.7 reduce-scatter.26

commit v2 on v1

v2 whole, which is shorter than its diff:
```python
import functools
import math

import jax
import jax.numpy as jnp
from jax import lax
from jax.experimental import pallas as pl
from jax.experimental.pallas import tpu as pltpu
from jax.sharding import Mesh, PartitionSpec as P


ROTARY_DIM = 64
LN_EPS = 1e-5
LANES = 128
PIECES = 2
MASKED = -1e30


def layer_norm(hidden_rows, gain_vec, bias_vec):
    rows_f32 = hidden_rows.astype(jnp.float32)
    row_mean = jnp.mean(rows_f32, axis=-1, keepdims=True)
    centered = rows_f32 - row_mean
    row_var = jnp.mean(centered * centered, axis=-1, keepdims=True)
    return (centered * lax.rsqrt(row_var + LN_EPS) * gain_vec + bias_vec).astype(jnp.bfloat16)


def norm_body(has_partial, waits, *refs):
    inputs = 5 if has_partial else 3
    refs = refs[:inputs] + refs[inputs + waits :]
    if has_partial:
        held_ref, part_ref, shift_ref, gain_ref, bias_ref, new_ref, normed_ref = refs
        rows = held_ref[...].astype(jnp.float32) + part_ref[...].astype(jnp.float32) + shift_ref[...]
        new_ref[...] = rows.astype(new_ref.dtype)
        rows = new_ref[...]
    else:
        held_ref, gain_ref, bias_ref, normed_ref = refs
        rows = held_ref[...]
    normed_ref[...] = layer_norm(rows, gain_ref[...], bias_ref[...])


def residual_norm(held, at, rows, layer, gain, bias, partial=None, shift=None, after=()):
    prompt, first = at
    d = held.shape[-1]
    block = min(rows, 128)
    held_spec = pl.BlockSpec((None, block, d), lambda i: (prompt, first // block + i, 0))
    row_spec = pl.BlockSpec((block, d), lambda i: (i, 0))
    new_spec = pl.BlockSpec((None, block, d), lambda i: (0, i, 0))
    vec_spec = lambda l: pl.BlockSpec((None, 1, d), lambda i: (l, 0, 0))
    out = [jax.ShapeDtypeStruct((rows, d), jnp.bfloat16)]
    vec = lambda a: a[:, None, :]
    operands, specs, out_specs = [held], [held_spec], [row_spec]
    if partial is not None:
        operands += [partial, vec(shift)]
        specs += [row_spec, vec_spec(layer - 1)]
        out = [jax.ShapeDtypeStruct((1, rows, d), jnp.bfloat16)] + out
        out_specs = [new_spec] + out_specs
    return pl.pallas_call(
        functools.partial(norm_body, partial is not None, len(after)),
        grid=(rows // block,),
        in_specs=specs + [vec_spec(layer)] * 2 + [pl.BlockSpec(memory_space=pl.ANY)] * len(after),
        out_specs=out_specs,
        out_shape=out,
        name="residual_norm",
        cost_estimate=pl.CostEstimate(flops=12 * rows * d, bytes_accessed=8 * rows * d, transcendentals=0),
    )(*operands, vec(gain), vec(bias), *after)


def last_body(held_ref, part_ref, shift_ref, *rest):
    rows = held_ref[...].astype(jnp.float32) + part_ref[...].astype(jnp.float32) + shift_ref[...]
    rest[-1][...] = rows.astype(rest[-1].dtype)


def last_residual(result, batch, prompt, held, first, partial, shift):
    rows, d = partial.shape
    total = held.shape[1]
    block = min(rows, 128)
    row_spec = pl.BlockSpec((block, d), lambda i: (i, 0))
    out_spec = pl.BlockSpec((None, block, d), lambda i: (prompt, first // block + i, 0))
    made = [] if result is None else [result]
    return pl.pallas_call(
        last_body,
        grid=(rows // block,),
        in_specs=[pl.BlockSpec((None, block, d), lambda i: (0, first // block + i, 0)), row_spec, pl.BlockSpec((1, d), lambda i: (0, 0))] + [pl.BlockSpec(memory_space=pl.ANY)] * len(made),
        out_specs=out_spec,
        out_shape=jax.ShapeDtypeStruct((batch, total, d), jnp.bfloat16),
        input_output_aliases={3: 0} if made else {},
        name="last_residual",
        cost_estimate=pl.CostEstimate(flops=2 * rows * d, bytes_accessed=6 * rows * d, transcendentals=0),
    )(held, partial, shift[None, :], *made)


def rotary_lanes(seq_full):
    positions = jnp.arange(seq_full).astype(jnp.float32)
    inv_freq = 10000.0 ** (-jnp.arange(0, ROTARY_DIM, 2).astype(jnp.float32) / ROTARY_DIM)
    angles = positions[:, None] * jnp.repeat(inv_freq, 2)[None, :]
    rest = ((0, 0), (0, LANES - ROTARY_DIM))
    cos_tab = jnp.pad(jnp.cos(angles), rest, constant_values=1.0)
    sin_tab = jnp.pad(jnp.sin(angles), rest)
    even = (jnp.arange(LANES) % 2 == 0)[None, :]
    return cos_tab, jnp.where(even, -sin_tab, 0.0), jnp.where(even, 0.0, sin_tab)


def qkv_body(heads, head_dim, count, *refs):
    pieces = refs[:count]
    wq_ref, wk_ref, wv_ref, cos_ref, up_ref, down_ref = refs[count : count + 6]
    q_ref, k_ref, v_ref = refs[-3:]
    rows = jnp.concatenate([piece[...] for piece in pieces], axis=0)
    assert math.frexp(head_dim**-0.5)[0] == 0.5
    for w_ref, o_ref, turned in ((wq_ref, q_ref, True), (wk_ref, k_ref, True), (wv_ref, v_ref, False)):
        projected = jnp.dot(rows, w_ref[...], preferred_element_type=jnp.float32)
        if o_ref is q_ref:
            projected = projected * head_dim**-0.5
        for head in range(heads):
            lo = head * head_dim
            if turned:
                first = projected[:, lo : lo + LANES]
                first = first * cos_ref[...] + pltpu.roll(first, LANES - 1, 1) * up_ref[...] + pltpu.roll(first, 1, 1) * down_ref[...]
                o_ref[head, :, :LANES] = first.astype(o_ref.dtype)
                o_ref[head, :, LANES:] = projected[:, lo + LANES : lo + head_dim].astype(o_ref.dtype)
            else:
                o_ref[head] = projected[:, lo : lo + head_dim].astype(o_ref.dtype)


def project_qkv(pieces, wq, wk, wv, tables, layer, heads, head_dim, after):
    devices, rows, d = pieces[0].shape
    block = rows * len(pieces)
    width = heads * head_dim
    weight_spec = pl.BlockSpec((None, d, width), lambda i: (layer, 0, 0), pipeline_mode=pl.Buffered(1))
    table_spec = pl.BlockSpec((block, LANES), lambda i: (i, 0))
    out_spec = pl.BlockSpec((heads, block, head_dim), lambda i: (0, i, 0))
    out = jax.ShapeDtypeStruct((heads, devices * block, head_dim), jnp.bfloat16)
    return pl.pallas_call(
        functools.partial(qkv_body, heads, head_dim, len(pieces)),
        grid=(devices,),
        in_specs=[pl.BlockSpec((None, rows, d), lambda i: (i, 0, 0))] * len(pieces) + [weight_spec] * 3 + [table_spec] * 3 + [pl.BlockSpec(memory_space=pl.ANY)] * len(after),
        out_specs=[out_spec] * 3,
        out_shape=[out] * 3,
        name="project_qkv",
        cost_estimate=pl.CostEstimate(flops=6 * devices * block * d * width, bytes_accessed=2 * devices * block * d + 6 * d * width + 6 * devices * block * width, transcendentals=0),
        compiler_params=pltpu.CompilerParams(dimension_semantics=("arbitrary",), vmem_limit_bytes=60 * 1024 * 1024),
    )(*pieces, wq, wk, wv, *tables, *after)


def attention_body(heads, head_dim, block, batch_idx, lengths_ref, q_ref, k_ref, v_ref, *rest):
    o_ref = rest[-1]
    length = lengths_ref[batch_idx]
    q_idx = pl.program_id(0)
    whole = jnp.minimum(q_idx, length // block)

    def scores_of(head, k_idx):
        keys = k_ref[head, pl.ds(pl.multiple_of(k_idx * block, block), block), :]
        return lax.dot_general(q_ref[head], keys, (((1,), (1,)), ((), ())), preferred_element_type=jnp.float32)

    def values_of(head, k_idx):
        return v_ref[head, pl.ds(pl.multiple_of(k_idx * block, block), block), :]

    q_pos = q_idx * block + lax.broadcasted_iota(jnp.int32, (block, block), 0)
    k_pos = whole * block + lax.broadcasted_iota(jnp.int32, (block, block), 1)
    allowed = (k_pos <= q_pos) & (k_pos < length)
    state = []
    for head, scores in enumerate([scores_of(head, whole) for head in range(heads)]):
        scores = jnp.where(allowed, scores, MASKED)
        top = jnp.max(scores, axis=1, keepdims=True)
        probs = jnp.exp(scores - top)
        total = jnp.sum(probs, axis=1, keepdims=True)
        acc = jnp.dot(probs.astype(jnp.bfloat16), values_of(head, whole), preferred_element_type=jnp.float32)
        state.append((top, total, acc))

    def step(k_idx, state):
        out = []
        all_scores = [scores_of(head, k_idx) for head in range(heads)]
        for head, (scores, (top, total, acc)) in enumerate(zip(all_scores, state)):
            new_top = jnp.maximum(top, jnp.max(scores, axis=1, keepdims=True))
            probs = jnp.exp(scores - new_top)
            shrink = jnp.exp(top - new_top)
            total = total * shrink + jnp.sum(probs, axis=1, keepdims=True)
            acc = acc * shrink + jnp.dot(probs.astype(jnp.bfloat16), values_of(head, k_idx), preferred_element_type=jnp.float32)
            out.append((new_top, total, acc))
        return tuple(out)

    state = lax.fori_loop(0, whole, step, tuple(state))
    for head, (_, total, acc) in enumerate(state):
        o_ref[:, head * head_dim : (head + 1) * head_dim] = (acc / total).astype(o_ref.dtype)


def causal_attention(lengths, query_all, keys_all, values_all, batch_idx, block, after=()):
    heads, seq, head_dim = query_all.shape
    whole_spec = pl.BlockSpec((heads, seq, head_dim), lambda i, *_: (0, 0, 0))
    return pl.pallas_call(
        functools.partial(attention_body, heads, head_dim, block, batch_idx),
        grid_spec=pltpu.PrefetchScalarGridSpec(
            num_scalar_prefetch=1,
            grid=(seq // block,),
            in_specs=[pl.BlockSpec((heads, block, head_dim), lambda i, *_: (0, i, 0)), whole_spec, whole_spec] + [pl.BlockSpec(memory_space=pl.ANY)] * len(after),
            out_specs=pl.BlockSpec((block, heads * head_dim), lambda i, *_: (i, 0)),
        ),
        out_shape=jax.ShapeDtypeStruct((seq, heads * head_dim), jnp.bfloat16),
        name="causal_attention",
        cost_estimate=pl.CostEstimate(flops=4 * heads * seq * seq * head_dim, bytes_accessed=8 * heads * seq * head_dim, transcendentals=heads * seq * seq // 2),
        compiler_params=pltpu.CompilerParams(dimension_semantics=("arbitrary",), vmem_limit_bytes=60 * 1024 * 1024),
    )(lengths, query_all, keys_all, values_all, *after)


def out_body(ctx_ref, fc_ref, wo_ref, w_ref, o_ref, send_ref, recv_ref, send_sem, recv_sem):
    n, side, h = (pl.program_id(i) for i in range(3))
    sibling = 1 - lax.axis_index("core")
    slots = recv_ref.shape[0] - 1

    def exchange(half):
        slot = n * 2 + half
        return pltpu.make_async_remote_copy(
            src_ref=send_ref.at[half], dst_ref=recv_ref.at[slot], send_sem=send_sem.at[half], recv_sem=recv_sem.at[slot], device_id={"core": sibling}, device_id_type=pl.DeviceIdType.MESH
        )

    @pl.when((n == 0) & (side == 0) & (h == 0))
    def _():
        recv_ref[slots] = jnp.zeros(recv_ref.shape[1:], recv_ref.dtype)
        barrier = pltpu.get_barrier_semaphore()
        pl.semaphore_signal(barrier, inc=1, device_id={"core": sibling}, device_id_type=pl.DeviceIdType.MESH)
        pl.semaphore_wait(barrier, 1)

    @pl.when((side == 0) & (h == 1))
    def _():
        exchange(0).start()

    @pl.when((side == 1) & (h == 0))
    def _():
        exchange(1).start()
        exchange(0).wait()

    @pl.when((side == 1) & (h == 1))
    def _():
        exchange(1).wait()

    groups, rows, width = ctx_ref.shape
    cols = o_ref.shape[-1] // 4
    fc = fc_ref[...].reshape(groups * rows, fc_ref.shape[-1])
    ctx = ctx_ref[...].reshape(groups * rows, width)
    slot = jnp.where(side == 1, n * 2 + h, slots)
    for part in range(4):
        at = slice(part * cols, (part + 1) * cols)
        total = jnp.dot(fc, w_ref[:, at], preferred_element_type=jnp.float32)
        total += jnp.dot(ctx, wo_ref[:, at], preferred_element_type=jnp.float32)
        send_ref[h, :, at] = total.astype(send_ref.dtype)
        both = total + recv_ref[slot, :, at].astype(jnp.float32)
        o_ref[:, :, at] = both.astype(o_ref.dtype).reshape(groups, rows, cols)


def project_out(context, fc_hidden, wo, w_out, layer, piece, collective_id):
    chips, cores, _, rows, width = context.shape
    ff = fc_hidden.shape[-1]
    d = wo.shape[-1]
    group = chips // 2
    cols = 1024
    block = group * rows
    slots = d // cols * 2

    def core_of(side):
        return lax.rem(lax.axis_index("core") + 1 + side, 2)

    work = chips * cores * rows
    return pl.pallas_call(
        out_body,
        grid=(d // cols, cores, 2),
        in_specs=[
            pl.BlockSpec((group, None, None, rows, width), lambda n, s, h: (h, core_of(s), piece, 0, 0)),
            pl.BlockSpec((group, None, None, rows, ff), lambda n, s, h: (h, core_of(s), 0, 0, 0)),
            pl.BlockSpec((None, width, cols), lambda n, s, h: (layer, 0, n)),
            pl.BlockSpec((None, ff, cols), lambda n, s, h: (layer, 0, n)),
        ],
        out_specs=pl.BlockSpec((group, rows, cols), lambda n, s, h: (h * s, 0, n)),
        out_shape=jax.ShapeDtypeStruct((chips, rows, d), jnp.bfloat16),
        scratch_shapes=[
            pltpu.VMEM((2, block, cols), jnp.bfloat16),
            pltpu.VMEM((slots + 1, block, cols), jnp.bfloat16),
            pltpu.SemaphoreType.DMA((2,)),
            pltpu.SemaphoreType.DMA((slots,)),
        ],
        name="project_out",
        cost_estimate=pl.CostEstimate(flops=2 * work * (ff + width) * d, bytes_accessed=2 * (work * (ff + width + d) + (ff + width) * d), transcendentals=0),
        compiler_params=pltpu.CompilerParams(dimension_semantics=("arbitrary",) * 3, vmem_limit_bytes=63 * 1024 * 1024, collective_id=collective_id, has_side_effects=True),
    )(context, fc_hidden, wo, w_out)


def solution(mesh):
    tp_size = mesh.shape["tp"]
    mesh = Mesh(mesh.devices.reshape(mesh.shape["dp"], tp_size // 2, 2), ("dp", "chip", "core"))
    tp = ("chip", "core")

    def device_step(hidden, lengths, ln_gain, ln_bias, w_query, w_key, w_value, w_attn_out, w_fc_in, b_fc_in, w_fc_out, b_fc_out):
        batch, rows_own, d = hidden.shape
        layers, _, heads, head_dim = w_query.shape
        seq_full = rows_own * tp_size
        tables = rotary_lanes(seq_full)
        wq, wk, wv = (w.reshape(layers, d, heads * head_dim) for w in (w_query, w_key, w_value))
        wo = w_attn_out.reshape(layers, heads * head_dim, d)
        chips = tp_size // 2

        def pieces_of(layer, b):
            return PIECES if (layer, b) in ((0, 0), (layers - 1, batch - 1)) else 1

        def gather(normed, layer, b):
            count = pieces_of(layer, b)
            rows = rows_own // count
            if len(normed) < count:
                normed = [normed[0][piece * rows : (piece + 1) * rows] for piece in range(count)]
            gathered = []
            for piece in range(count):
                gathered.append(lax.all_gather(normed[piece], tp, axis=0))
            return gathered

        def fc_in(rows, layer):
            return jax.nn.gelu(jnp.einsum("ntd,df->ntf", rows, w_fc_in[layer], preferred_element_type=jnp.float32) + b_fc_in[layer], approximate=True).astype(jnp.bfloat16)

        stages = [(layer, b) for layer in range(layers) for b in range(batch)]
        held = [(hidden, b) for b in range(batch)]
        normed = []
        for b in range(batch):
            count = pieces_of(0, b)
            rows = rows_own // count
            normed.append([residual_norm(hidden, (b, piece * rows), rows, 0, ln_gain, ln_bias, after=normed[-1] if normed else ())[0] for piece in range(count)])
        gathered = [gather(normed[b], 0, b) for b in range(batch)]
        cache_k = []
        cache_v = []
        result = None
        waiting = None
        for layer, b in stages:
            pieces = pieces_of(layer, b)
            rows = rows_own // pieces
            first_fc = fc_in(gathered[b][0], layer)

            def qkv(after):
                return project_qkv(gathered[b], wq, wk, wv, tables, layer, heads, head_dim, after)

            early = waiting is None or pieces_of(*waiting[:2]) > 1
            if not early:
                query_all, keys_all, values_all = qkv([first_fc])
            moved = []
            if waiting is not None:
                up, prompt, sums = waiting
                if up < layers - 1:
                    after = [first_fc] if early else [first_fc, query_all]
                    array, place = held[prompt]
                    new, normed_rows = residual_norm(array, (place, 0), rows_own, up + 1, ln_gain, ln_bias, jnp.concatenate(sums, axis=0), b_fc_out, after)
                    held[prompt] = (new, 0)
                    gathered[prompt] = gather([normed_rows], up + 1, prompt)
                    moved = [normed_rows]
                else:
                    result = last_residual(result, batch, prompt, held[prompt][0], 0, jnp.concatenate(sums, axis=0), b_fc_out[up])
            if early:
                query_all, keys_all, values_all = qkv([first_fc] + moved)
            cache_k.append(keys_all)
            cache_v.append(values_all)
            context = causal_attention(lengths, query_all, keys_all, values_all, b, rows_own, moved)
            context = context.reshape(chips, 2, pieces, rows, heads * head_dim)
            sums = []
            part = None
            for piece in range(pieces):
                if piece == 0:
                    fc = first_fc
                else:
                    source, _ = lax.optimization_barrier((gathered[b][piece], part))
                    fc = fc_in(source, layer)
                fc = fc.reshape(chips, 2, 1, rows, -1)
                part = project_out(context, fc, wo, w_fc_out, layer, piece, (layer * batch + b) * PIECES + piece)
                sums.append(lax.psum_scatter(part, "chip", scatter_dimension=0))
            waiting = (layer, b, sums)
        layer, b, sums = waiting
        for piece, part in enumerate(sums):
            result = last_residual(result, batch, b, held[b][0], piece * (rows_own // len(sums)), part, b_fc_out[layer])
        cache_shape = (layers, batch, heads, seq_full, head_dim)
        return result, jnp.stack(cache_k).reshape(cache_shape), jnp.stack(cache_v).reshape(cache_shape)

    head_cols = P(None, None, tp, None)
    cache_spec = P(None, "dp", tp, None, None)
    hidden_spec = P("dp", tp, None)
    return jax.shard_map(device_step, mesh=mesh, in_specs=(hidden_spec, P("dp"), P(), P(), head_cols, head_cols, head_cols, P(None, tp, None, None), P(None, None, tp), P(None, tp), P(None, tp, None), P()), out_specs=(hidden_spec, cache_spec, cache_spec), check_vma=False)
```

time: 1910 us -> 1740 us (0.911)
  waiting for transfers between devices: 574 us -> 425 us
    unnamed x18, waiting for transfers between devices: 303 us -> 205 us
    all_gather x6, waiting for transfers between devices: 271 us -> 220 us  [gather(): gathered.append(lax.all_gather(normed[piece], tp, axis=0))]
    pallas_call x14 -> x18, Pallas kernels: 697 us -> 709 us  [the longest x6 413 us: project_out(): pl.pallas_call(out_body, grid=(d // cols, cores, 2), in_specs=[pl.BlockSp...]
  transfers between devices with their start and end apart: 12 -> 12, of which waited for: 10 -> 7; matrix products, arithmetic and copies ran while one was open for 16% -> 18% of each run, Pallas kernels for 28% -> 34%
where the time goes in v2:
time: 1740 us; the launch traced here: 1730 us
  Pallas kernels  843 us (48%)
  waiting for transfers between devices  425 us (24%)
  matrix products  354 us (20%)
  local copies, waits for them, and re-layouts  55 us (3%)
  other arithmetic  38.6 us (2%)
    pallas_call x6, Pallas kernels, project_out(): pl.pallas_call(out_body, grid=(d // cols, cores, 2), in_specs=[pl.BlockSp...  413 us
    dot_general x6, matrix products, fc_in(): jnp.einsum('ntd,df->ntf', rows, w_fc_in[layer], preferred_element_type=jn...  354 us
    pallas_call x4, Pallas kernels, project_qkv(): pl.pallas_call(functools.partial(qkv_body, heads, head_dim, len(pieces)),...  249 us
    all_gather x6, waiting for transfers between devices, gather(): gathered.append(lax.all_gather(normed[piece], tp, axis=0))  220 us
    unnamed x18, waiting for transfers between devices  205 us
    pallas_call x4, Pallas kernels, causal_attention(): pl.pallas_call(functools.partial(attention_body, heads, head_dim, block,...  134 us
    reshape x3, local copies, waits for them, and re-layouts, device_step(): w.reshape(layers, d, heads * head_dim)  42.8 us
  transfers between devices with their start and end apart: 12, of which 7 were waited for; matrix products, arithmetic and copies ran while one was open for 18% of the time, Pallas kernels for 34%

profile of v2, /device:TPU:0, one launch (start us, length us, event | category | flops | bytes accessed | tf_op | source)
XLA Modules:
  0.0 1731.1 jit_solution(11803186433225863754)
XLA Ops:
  7.2 1.4 broadcast_in_dim.47.refs_1_.refs_3_
  8.6 1.4 broadcast_in_dim.48.refs_2_.refs_4_
  10.0 4.3 residual_norm.5.refs_3_
  14.3 0.0 all-gather.17.cloned.1.call-start
  14.4 4.3 residual_norm.6.refs_4_
  18.7 0.3 reduce-scatter.21.cloned.1.call-start
  19.0 0.1 broadcast_in_dim.49
  19.1 0.1 mul.106
  19.2 14.4 reshape.71.refs_2_.refs_1_
  33.6 14.0 reshape.72.refs_3_.refs_2_
  47.6 14.4 reshape.73.refs_4_.refs_3_
  62.0 7.3 multiply_sine_fusion
  69.3 1.5 pad.8.refs_5_.refs_4_
  70.8 0.6 fusion.74
  71.4 2.4 pad_select_fusion
  73.8 27.6 %all-gather.15.cloned.1.call-done = bf16[2048,4096]{1,0:T(8,128)(2,1)} async-done(((bf16[256,4096]{1,0:T(8,128)(2,1)}), bf16[2048,4096]{1,0:T(8,128)(2,1)}) %all-gather.15.cloned.1.call-update) | async-done | bytes 16777232 | tf_op jit(solution)/shard_map/all_gather | solution.py:309
  101.4 46.2 %fusion.23.refs_8_ = bf16[8,256,2048]{2,1,0:T(8,128)(2,1)} fusion(f32[2048]{0:T(1024)S(1)} %bitcast.99, bf16[8,256,4096]{2,1,0:T(8,128)(2,1)} %bitcast.108, bf16[2,4096,2048]{2,1,0:T(8,128)(2,1)} %param.20), kind=kOutput, calls=%fused_computation.29 | convolution fusion | flops 34401681408 | bytes 41951232 | tf_op jit(solution)/shard_map/ntd,df->ntf/dot_general | solution.py:313
  147.6 39.8 %all-gather.17.cloned.1.call-done = bf16[2048,4096]{1,0:T(8,128)(2,1)} async-done(((bf16[256,4096]{1,0:T(8,128)(2,1)}), bf16[2048,4096]{1,0:T(8,128)(2,1)}) %all-gather.17.cloned.1.call-update) | async-done | bytes 16777232 | tf_op jit(solution)/shard_map/all_gather | solution.py:309
  187.5 62.2 %project_qkv.4 = (bf16[2,4096,256]{2,1,0:T(8,128)(2,1)}, bf16[2,4096,256]{2,1,0:T(8,128)(2,1)}, bf16[2,4096,256]{2,1,0:T(8,128)(2,1)}) custom-call(bf16[8,256,4096]{2,1,0:T(8,128)(2,1)} %bitcast.109, bf16[8,256,4096]{2,1,0:T(8,128)(2,1)} %bitcast.110, bf16[2,4096,512]{2,1,0:T(8,128)(2,1)} %reshape.71.refs_2_.refs_1_, ...), custom_call_target="tpu_custom_call" | custom-call | flops 51539607552 | bytes 58720256 | tf_op jit(solution)/shard_map/project_qkv/pallas_call | solution.py:132
  249.6 50.0 %causal_attention.4 = bf16[4096,512]{1,0:T(8,128)(2,1)} custom-call(s32[2]{0:T(128)} %lengths_ref.7, bf16[2,4096,256]{2,1,0:T(8,128)(2,1)} %get-tuple-element.21.q_ref, bf16[2,4096,256]{2,1,0:T(8,128)(2,1)} %get-tuple-element.22.k_ref, bf16[2,4096,256]{2,1,0:T(8,128)(2,1)} %get-tuple-element.23.v_ref), custom_call_target="tpu_custom_call" | custom-call | flops 34359738368 | bytes 16777216 | tf_op jit(solution)/shard_map/causal_attention/pallas_call | solution.py:189
  299.6 54.3 %project_out.6 = bf16[4,256,4096]{2,1,0:T(8,128)(2,1)} custom-call(bf16[4,2,2,256,512]{4,3,2,1,0:T(8,128)(2,1)} %bitcast.126, bf16[4,2,1,256,2048]{4,3,2,1,0:T(8,128)(2,1)} %bitcast.121, bf16[2,512,4096]{2,1,0:T(8,128)(2,1)} %bitcast.114, bf16[2,2048,4096]{2,1,0:T(8,128)(2,1)} %w_ref.11), custom_call_target="tpu_custom_call" | custom-call | flops 42949672960 | bytes 48234496 | tf_op jit(solution)/shard_map/project_out/pallas_call | solution.py:262
  353.9 45.6 %fusion.31 = bf16[8,256,2048]{2,1,0:T(8,128)(2,1)} fusion(f32[2048]{0:T(1024)S(1)} %bitcast.100, bf16[8,256,4096]{2,1,0:T(8,128)(2,1)} %bitcast.111, bf16[2,4096,2048]{2,1,0:T(8,128)(2,1)} %param.20), kind=kOutput, calls=%fused_computation.37 | convolution fusion | flops 34401681408 | bytes 41951232 | tf_op jit(solution)/shard_map/ntd,df->ntf/dot_general | solution.py:313
  399.6 54.6 %project_out.7 = bf16[4,256,4096]{2,1,0:T(8,128)(2,1)} custom-call(bf16[4,2,2,256,512]{4,3,2,1,0:T(8,128)(2,1)} %bitcast.127, bf16[4,2,1,256,2048]{4,3,2,1,0:T(8,128)(2,1)} %bitcast.123, bf16[2,512,4096]{2,1,0:T(8,128)(2,1)} %bitcast.115, bf16[2,2048,4096]{2,1,0:T(8,128)(2,1)} %w_ref.11), custom_call_target="tpu_custom_call" | custom-call | flops 42949672960 | bytes 48234496 | tf_op jit(solution)/shard_map/project_out/pallas_call | solution.py:262
  454.2 0.0 reduce-scatter.19.cloned.1.call-start
  454.2 0.5 reduce-scatter.19.cloned.1.call-update
  454.8 7.2 residual_norm.7
  462.0 0.0 all-gather.19.cloned.1.call-start
  462.1 0.6 broadcast_in_dim.52.refs_2_
  462.7 72.4 %reduce-scatter.21.cloned.1.call-done = bf16[1,256,4096]{2,1,0:T(8,128)(2,1)} async-done(((bf16[4,256,4096]{2,1,0:T(8,128)(2,1)}), bf16[1,256,4096]{2,1,0:T(8,128)(2,1)}) %reduce-scatter.21.cloned.1.call-update) | async-done | bytes 2097168
  535.1 83.6 %reduce-scatter.19.cloned.1.call-done = bf16[1,256,4096]{2,1,0:T(8,128)(2,1)} async-done(((bf16[4,256,4096]{2,1,0:T(8,128)(2,1)}), bf16[1,256,4096]{2,1,0:T(8,128)(2,1)}) %reduce-scatter.19.cloned.1.call-update) | async-done | bytes 2097168
  618.7 4.7 pad_maximum_fusion.2.refs_1_
  623.4 152.7 %all-gather.13.cloned.1.call-done = bf16[4096,4096]{1,0:T(8,128)(2,1)} async-done(((bf16[512,4096]{1,0:T(8,128)(2,1)}), bf16[4096,4096]{1,0:T(8,128)(2,1)}) %all-gather.13.cloned.1.call-update) | async-done | bytes 33554448 | tf_op jit(solution)/shard_map/all_gather | solution.py:309
  776.1 84.1 %fusion.7.refs_5_.refs_7_ = bf16[8,512,2048]{2,1,0:T(8,128)(2,1)} fusion(bf16[8,512,4096]{2,1,0:T(8,128)(2,1)} %bitcast.102, f32[2048]{0:T(1024)S(1)} %bitcast.101, bf16[2,4096,2048]{2,1,0:T(8,128)(2,1)} %param.20), kind=kOutput, calls=%fused_computation.9 | convolution fusion | flops 68803362816 | bytes 67117056 | tf_op jit(solution)/shard_map/ntd,df->ntf/dot_general | solution.py:313
  860.2 9.0 residual_norm.8
  869.3 0.0 reduce-scatter.23.cloned.1.call-start
  869.3 63.3 %project_qkv.5 = (bf16[2,4096,256]{2,1,0:T(8,128)(2,1)}, bf16[2,4096,256]{2,1,0:T(8,128)(2,1)}, bf16[2,4096,256]{2,1,0:T(8,128)(2,1)}) custom-call(bf16[8,512,4096]{2,1,0:T(8,128)(2,1)} %bitcast.103, bf16[2,4096,512]{2,1,0:T(8,128)(2,1)} %reshape.71.refs_2_.refs_1_, bf16[2,4096,512]{2,1,0:T(8,128)(2,1)} %reshape.72.refs_3_.refs_2_, ...), custom_call_target="tpu_custom_call" | custom-call | flops 51539607552 | bytes 58720256 | tf_op jit(solution)/shard_map/project_qkv/pallas_call | solution.py:132
  932.6 16.9 causal_attention.5
  949.5 97.0 %project_out.8 = bf16[4,512,4096]{2,1,0:T(8,128)(2,1)} custom-call(bf16[4,2,1,512,512]{4,3,2,1,0:T(8,128)(2,1)} %bitcast.129, bf16[4,2,1,512,2048]{4,3,2,1,0:T(8,128)(2,1)} %bitcast.81, bf16[2,512,4096]{2,1,0:T(8,128)(2,1)} %bitcast.116, bf16[2,2048,4096]{2,1,0:T(8,128)(2,1)} %w_ref.11), custom_call_target="tpu_custom_call" | custom-call | flops 85899345920 | bytes 75497472 | tf_op jit(solution)/shard_map/project_out/pallas_call | solution.py:262
  1046.6 0.0 all-gather.21.cloned.1.call-start
  1046.7 0.6 copy-done.7
  1047.3 85.2 %fusion.15.refs_7_.refs_5_ = bf16[8,512,2048]{2,1,0:T(8,128)(2,1)} fusion(bf16[8,512,4096]{2,1,0:T(8,128)(2,1)} %bitcast.104, f32[2048]{0:T(1024)S(1)} %bitcast.96, bf16[2,4096,2048]{2,1,0:T(8,128)(2,1)} %param.20), kind=kOutput, calls=%fused_computation.17 | convolution fusion | flops 68803362816 | bytes 67117056 | tf_op jit(solution)/shard_map/ntd,df->ntf/dot_general | solution.py:313
  1132.5 61.3 %project_qkv.6 = (bf16[2,4096,256]{2,1,0:T(8,128)(2,1)}, bf16[2,4096,256]{2,1,0:T(8,128)(2,1)}, bf16[2,4096,256]{2,1,0:T(8,128)(2,1)}) custom-call(bf16[8,512,4096]{2,1,0:T(8,128)(2,1)} %bitcast.105, bf16[2,4096,512]{2,1,0:T(8,128)(2,1)} %reshape.71.refs_2_.refs_1_, bf16[2,4096,512]{2,1,0:T(8,128)(2,1)} %reshape.72.refs_3_.refs_2_, ...), custom_call_target="tpu_custom_call" | custom-call | flops 51539607552 | bytes 58720256 | tf_op jit(solution)/shard_map/project_qkv/pallas_call | solution.py:132
  1193.8 2.0 reduce-scatter.23.cloned.1.call-done
  1195.8 9.2 residual_norm.9
  1204.9 4.7 fusion.73
  1209.7 0.7 all-gather.23.cloned.1.call-update
  1210.4 50.4 %causal_attention.7 = bf16[4096,512]{1,0:T(8,128)(2,1)} custom-call(s32[2]{0:T(128)} %lengths_ref.7, bf16[2,4096,256]{2,1,0:T(8,128)(2,1)} %get-tuple-element.29.refs_6_.q_ref, bf16[2,4096,256]{2,1,0:T(8,128)(2,1)} %get-tuple-element.37.k_ref, bf16[2,4096,256]{2,1,0:T(8,128)(2,1)} %get-tuple-element.38.v_ref, bf16[512,4096]{1,0:T(8,128)(2,1)} %get-tuple-element.31.rest_0_), custom_call_target="tpu_custom_call" | custom-call | flops 34359738368 | bytes 16777216 | tf_op jit(solution)/shard_map/causal_attention/pallas_call | solution.py:189
  1260.8 97.3 %project_out.11 = bf16[4,512,4096]{2,1,0:T(8,128)(2,1)} custom-call(bf16[4,2,1,512,512]{4,3,2,1,0:T(8,128)(2,1)} %bitcast.128, bf16[4,2,1,512,2048]{4,3,2,1,0:T(8,128)(2,1)} %bitcast.78, bf16[2,512,4096]{2,1,0:T(8,128)(2,1)} %bitcast.117, bf16[2,2048,4096]{2,1,0:T(8,128)(2,1)} %w_ref.11), custom_call_target="tpu_custom_call" | custom-call | flops 85899345920 | bytes 75497472 | tf_op jit(solution)/shard_map/project_out/pallas_call | solution.py:262
  1358.1 0.0 reduce-scatter.27.cloned.1.call-start
  1358.2 0.6 copy-done.8
  1358.8 45.9 %fusion.39.refs_8_ = bf16[8,256,2048]{2,1,0:T(8,128)(2,1)} fusion(f32[2048]{0:T(1024)S(1)} %bitcast.97, bf16[8,256,4096]{2,1,0:T(8,128)(2,1)} %bitcast.112, bf16[2,4096,2048]{2,1,0:T(8,128)(2,1)} %param.20), kind=kOutput, calls=%fused_computation.45 | convolution fusion | flops 34401681408 | bytes 41951232 | tf_op jit(solution)/shard_map/ntd,df->ntf/dot_general | solution.py:313
  1404.7 62.2 %project_qkv.7 = (bf16[2,4096,256]{2,1,0:T(8,128)(2,1)}, bf16[2,4096,256]{2,1,0:T(8,128)(2,1)}, bf16[2,4096,256]{2,1,0:T(8,128)(2,1)}) custom-call(bf16[8,256,4096]{2,1,0:T(8,128)(2,1)} %bitcast.113, bf16[8,256,4096]{2,1,0:T(8,128)(2,1)} %bitcast.106, bf16[2,4096,512]{2,1,0:T(8,128)(2,1)} %reshape.71.refs_2_.refs_1_, ...), custom_call_target="tpu_custom_call" | custom-call | flops 51539607552 | bytes 58720256 | tf_op jit(solution)/shard_map/project_qkv/pallas_call | solution.py:132
  1466.9 16.4 causal_attention.6
  1483.2 55.2 %project_out.9 = bf16[4,256,4096]{2,1,0:T(8,128)(2,1)} custom-call(bf16[4,2,2,256,512]{4,3,2,1,0:T(8,128)(2,1)} %bitcast.124, bf16[4,2,1,256,2048]{4,3,2,1,0:T(8,128)(2,1)} %bitcast.120, bf16[2,512,4096]{2,1,0:T(8,128)(2,1)} %bitcast.118, bf16[2,2048,4096]{2,1,0:T(8,128)(2,1)} %w_ref.11), custom_call_target="tpu_custom_call" | custom-call | flops 42949672960 | bytes 48234496 | tf_op jit(solution)/shard_map/project_out/pallas_call | solution.py:262
  1538.5 0.0 reduce-scatter.25.cloned.1.call-start
  1538.5 46.6 %fusion.47 = bf16[8,256,2048]{2,1,0:T(8,128)(2,1)} fusion(f32[2048]{0:T(1024)S(1)} %bitcast.98, bf16[8,256,4096]{2,1,0:T(8,128)(2,1)} %bitcast.107, bf16[2,4096,2048]{2,1,0:T(8,128)(2,1)} %param.20), kind=kOutput, calls=%fused_computation.53 | convolution fusion | flops 34401681408 | bytes 41951232 | tf_op jit(solution)/shard_map/ntd,df->ntf/dot_general | solution.py:313
  1585.1 54.6 %project_out.10 = bf16[4,256,4096]{2,1,0:T(8,128)(2,1)} custom-call(bf16[4,2,2,256,512]{4,3,2,1,0:T(8,128)(2,1)} %bitcast.125, bf16[4,2,1,256,2048]{4,3,2,1,0:T(8,128)(2,1)} %bitcast.122, bf16[2,512,4096]{2,1,0:T(8,128)(2,1)} %bitcast.119, bf16[2,2048,4096]{2,1,0:T(8,128)(2,1)} %w_ref.11), custom_call_target="tpu_custom_call" | custom-call | flops 42949672960 | bytes 48234496 | tf_op jit(solution)/shard_map/project_out/pallas_call | solution.py:262
  1639.7 0.6 slice.37.shift_ref
  1640.3 17.2 pad_maximum_fusion
  1657.5 7.0 pad_maximum_fusion.1
  1664.5 6.2 last_residual.3.rest_0_
  1670.7 3.7 last_residual.4.rest_0_
  1674.4 45.9 %reduce-scatter.25.cloned.1.call-done = bf16[1,256,4096]{2,1,0:T(8,128)(2,1)} async-done(((bf16[4,256,4096]{2,1,0:T(8,128)(2,1)}), bf16[1,256,4096]{2,1,0:T(8,128)(2,1)}) %reduce-scatter.25.cloned.1.call-update) | async-done | bytes 2097168
  1720.3 3.5 last_residual.5
  (38 shorter events, 0.4 us)
Async XLA Ops:
  7.2 94.3 %all-gather.15.cloned.1.call-start = ((), (), s32[]{:S(2)}) async-start(), calls=%async_computation.7 | async-start | bytes 18874368 | tf_op jit(solution)/shard_map/all_gather | solution.py:309
  14.3 173.1 %all-gather.17.cloned.1.call-start = ((), (), s32[]{:S(2)}) async-start(), calls=%async_computation.8 | async-start | bytes 18874368 | tf_op jit(solution)/shard_map/all_gather | solution.py:309
  18.7 516.4 %reduce-scatter.21.cloned.1.call-start = ((), (), s32[]{:S(2)}) async-start(), calls=%async_computation.13 | async-start | bytes 10485760
  47.6 23.2 %copy-start.6 = (f32[2,2048]{1,0:T(2,128)S(1)}, f32[2,2048]{1,0:T(2,128)}, u32[]{:S(2)}) copy-start(f32[2,2048]{1,0:T(2,128)} %param.21) | copy-start | bytes 49156
  454.2 7.9 copy-start.4
  454.2 164.5 %reduce-scatter.19.cloned.1.call-start = ((), (), s32[]{:S(2)}) async-start(), calls=%async_computation.12 | async-start | bytes 10485760
  454.8 321.3 %all-gather.13.cloned.1.call-start = ((), (), s32[]{:S(2)}) async-start(), calls=%async_computation.6 | async-start | bytes 37748736 | tf_op jit(solution)/shard_map/all_gather | solution.py:309
  462.0 584.6 %all-gather.19.cloned.1.call-start = ((), (), s32[]{:S(2)}) async-start(), calls=%async_computation.9 | async-start | bytes 37748736 | tf_op jit(solution)/shard_map/all_gather | solution.py:309
  869.3 326.5 %reduce-scatter.23.cloned.1.call-start = ((), (), s32[]{:S(2)}) async-start(), calls=%async_computation.14 | async-start | bytes 20971520
  1046.6 0.7 copy-start.7
  1046.6 311.6 %all-gather.21.cloned.1.call-start = ((), (), s32[]{:S(2)}) async-start(), calls=%async_computation.10 | async-start | bytes 18874368 | tf_op jit(solution)/shard_map/all_gather | solution.py:309
  1209.6 195.0 %all-gather.23.cloned.1.call-start = ((), (), s32[]{:S(2)}) async-start(), calls=%async_computation.11 | async-start | bytes 18874368 | tf_op jit(solution)/shard_map/all_gather | solution.py:309
  1210.4 454.2 %reduce-scatter.29.cloned.1.call-start = ((), (), s32[]{:S(2)}) async-start(), calls=%async_computation.17 | async-start | bytes 20971520
  1358.1 0.7 copy-start.8
  1358.1 312.6 %reduce-scatter.27.cloned.1.call-start = ((), (), s32[]{:S(2)}) async-start(), calls=%async_computation.16 | async-start | bytes 10485760
  1538.5 181.8 %reduce-scatter.25.cloned.1.call-start = ((), (), s32[]{:S(2)}) async-start(), calls=%async_computation.15 | async-start | bytes 10485760
  1585.1 54.6 %copy-start.5 = (f32[2,4096]{1,0:T(2,128)S(1)}, f32[2,4096]{1,0:T(2,128)}, u32[]{:S(2)}) copy-start(f32[2,4096]{1,0:T(2,128)} %param.23) | copy-start | bytes 98308
  1640.3 17.2 copy-start
  1640.3 17.2 copy-start.1
  1640.3 17.2 copy-start.2
  1640.3 17.2 copy-start.3
Sparse Core Ops, SparseCore 0:
  14.4 86.9 all-gather.14
  103.3 84.1 all-gather.16
  454.3 80.7 reduce-scatter.20
  537.9 80.7 reduce-scatter.18
  621.0 155.0 all-gather.12
  869.4 155.0 all-gather.18
  1046.7 148.9 reduce-scatter.22
  1209.8 84.1 all-gather.20
  1295.8 84.3 all-gather.22
  1383.1 148.1 reduce-scatter.28
  1538.6 80.1 reduce-scatter.26
  1639.8 80.4 reduce-scatter.24
